TPU v7x, 32 devices: a whole 2x2x4 slice. The times are simulated.
32 devices in a mesh: lat: 4 (over x, core), lon: 2 (over y), lev: 4 (over z).
Axes of the slice: x: 2, y: 2, z: 4, core: 2. Of those that a mesh axis runs over, the one named last changes fastest.
Arguments:
- outer_increment: bfloat16 [16, 256, 1024], P('lev', 'lat', 'lon'), may hold values from -6 to 6
- courant: bfloat16 [3, 16, 64, 256], P(None, 'lev', 'lat', 'lon'), may hold values from -0.29882812 to 0.29882812
- obs_column: int32 [16384], P(('lat', 'lon')), may hold values from 0 to 2047
- obs_level: int32 [16384], P(('lat', 'lon')), may hold values from 0 to 15
- obs_value: float32 [16384], P(('lat', 'lon')), may hold values from -6 to 6
Outputs:
- inner_state: float32 [16, 64, 256], P('lev', 'lat', 'lon')
- adjoint: float32 [16, 64, 256], P('lev', 'lat', 'lon')
- outer_next: bfloat16 [16, 256, 1024], P('lev', 'lat', 'lon')
Inputs may be any that keep to these rules, and one draw needn't show every extreme that they name: obs_column numbers a column of the 16 x 512 / 4 inner block of its latitude-longitude block, row by row.
All inputs are finite; a program needn't handle non-finite values.
Results may differ from a plain program's by a relative error of at most 0.001.
Values sent between devices are 32-bit elements; how exact they have to be, the bound alone decides.
A program may use at most 64 MiB of HBM per device.

v0:
```python
import jax
import jax.numpy as jnp
from jax import lax
from jax.sharding import PartitionSpec as P


def with_halo(array, sides, width, wrap):
    for axis, dim in sides:
        size, length = (lax.axis_size(axis), array.shape[dim])
        up = [(i, (i + 1) % size) for i in range(size if wrap else size - 1)]
        down = [(j, i) for i, j in up]
        last = lax.slice_in_dim(array, length - width, length, axis=dim)
        first = lax.slice_in_dim(array, 0, width, axis=dim)
        before = lax.ppermute(last, axis, up)
        after = lax.ppermute(first, axis, down)
        array = jnp.concatenate([before, array, after], axis=dim)
    return array


def extend_deep(field):
    wrapped = with_halo(field, (("lon", 3),), 2, True)
    return with_halo(wrapped, (("lat", 2), ("lev", 1)), 2, False)


def window_of(field, axis, shift):
    sizes = [field.shape[1] - 2, field.shape[2] - 2, field.shape[3] - 2]
    begins = [1, 1, 1]
    begins[axis - 1] = begins[axis - 1] + shift
    return field[
        :,
        begins[0] : begins[0] + sizes[0],
        begins[1] : begins[1] + sizes[1],
        begins[2] : begins[2] + sizes[2],
    ]


def advance(padded, speeds):
    numbers = window_of(speeds, 1, 0)
    result = (1.0 - jnp.sum(jnp.abs(numbers), axis=0, keepdims=True)) * window_of(padded, 1, 0)
    for direction in range(3):
        lower = jnp.maximum(numbers[direction : direction + 1], 0.0)
        upper = jnp.maximum(-numbers[direction : direction + 1], 0.0)
        result = (
            result
            + lower * window_of(padded, direction + 1, -1)
            + upper * window_of(padded, direction + 1, 1)
        )
    return result


def retreat(padded, speeds):
    numbers = window_of(speeds, 1, 0)
    result = (1.0 - jnp.sum(jnp.abs(numbers), axis=0, keepdims=True)) * window_of(padded, 1, 0)
    for direction in range(3):
        lower = jnp.maximum(speeds[direction : direction + 1], 0.0)
        upper = jnp.maximum(-speeds[direction : direction + 1], 0.0)
        result = (
            result
            + window_of(lower * padded, direction + 1, 1)
            + window_of(upper * padded, direction + 1, -1)
        )
    return result


def shards(outer_increment, courant, obs_column, obs_level, obs_value):
    levels_dev, rows, columns = outer_increment.shape
    inner_rows = rows // 4
    inner_cols = columns // 4
    owner = lax.iota(jnp.int32, columns)[:, None] // 4 == lax.iota(jnp.int32, inner_cols)[None, :]
    column_table = owner.astype(jnp.bfloat16)
    column_sums = jnp.dot(
        outer_increment.reshape(levels_dev * rows, columns),
        column_table,
        preferred_element_type=jnp.float32,
    )
    coarse = jnp.sum(column_sums.reshape(levels_dev, inner_rows, 4, inner_cols), axis=2) * 0.0625
    numbers = courant.astype(jnp.float32)
    stacked = jnp.concatenate([coarse[None], numbers], axis=0)
    widened = extend_deep(stacked)
    speeds = widened[1:]
    state = advance(widened[0:1], speeds)
    state = advance(state, window_of(speeds, 1, 0))
    lowest = lax.axis_index("lev") * levels_dev
    levels_held = state.shape[1]
    local_level = obs_level - lowest
    inside = (local_level >= 0) & (local_level < levels_held)
    flat = jnp.clip(local_level, 0, levels_held - 1) * (inner_rows * inner_cols) + obs_column
    innovation = jnp.where(inside, state.reshape(-1)[flat] - obs_value, 0.0)
    forcing = (
        jnp.zeros((levels_held * inner_rows * inner_cols,), jnp.float32).at[flat].add(innovation)
    )
    adjoint = forcing.reshape(1, levels_held, inner_rows, inner_cols)
    widened = extend_deep(adjoint)
    first = retreat(widened, speeds)
    level_index = lowest - 1 + lax.iota(jnp.int32, levels_dev + 2)
    row_index = lax.axis_index("lat") * inner_rows - 1 + lax.iota(jnp.int32, inner_rows + 2)
    level_keep = (level_index >= 0) & (level_index < lax.axis_size("lev") * levels_dev)
    row_keep = (row_index >= 0) & (row_index < lax.axis_size("lat") * inner_rows)
    keeper = level_keep[:, None, None] & row_keep[None, :, None]
    first = jnp.where(keeper[None], first, 0.0)
    adjoint = retreat(first, window_of(speeds, 1, 0))
    spread_table = jnp.transpose(owner).astype(jnp.float32)
    widened_cols = jnp.dot(
        adjoint[0].reshape(levels_dev * inner_rows, inner_cols),
        spread_table,
        precision=lax.Precision.HIGHEST,
        preferred_element_type=jnp.float32,
    )
    spread = jnp.broadcast_to(
        widened_cols.reshape(levels_dev, inner_rows, 1, columns),
        (levels_dev, inner_rows, 4, columns),
    ).reshape(levels_dev, rows, columns)
    outer_next = (outer_increment.astype(jnp.float32) - spread).astype(jnp.bfloat16)
    return (state[0], adjoint[0], outer_next)


def solution(mesh):
    placed = (
        P("lev", "lat", "lon"),
        P(None, "lev", "lat", "lon"),
        P(("lat", "lon")),
        P(("lat", "lon")),
        P(("lat", "lon")),
    )
    return jax.shard_map(
        shards,
        mesh=mesh,
        in_specs=placed,
        out_specs=(P("lev", "lat", "lon"), P("lev", "lat", "lon"), P("lev", "lat", "lon")),
        check_vma=False,
    )
```

profile of v0, /device:TPU:0, one launch (start us, length us, event | category | flops | bytes accessed | tf_op | source)
XLA Modules:
  0.0 80.0 jit_solution(10827559344927898365)
XLA Ops:
  0.6 1.3 %convolution_bitcast_fusion = f32[256,128]{0,1:T(8,128)S(1)} fusion(bf16[256,512]{1,0:T(8,128)(2,1)} %bitcast.30, s32[512]{0:T(512)S(1)} %add_select_fusion), kind=kOutput, calls=%fused_computation.2 | convolution fusion | flops 33685504 | bytes 395264 | tf_op jit(solution)/shard_map/dot_general | solution.py:71
  2.1 0.8 copy-done.2
  3.0 3.1 %collective-permute-start = (f32[4,4,16,2]{3,2,1,0:T(8,128)S(1)}, f32[4,4,16,2]{3,2,1,0:T(8,128)S(1)}, u32[]{:S(2)}, u32[]{:S(2)}) collective-permute-start(f32[4,4,16,2]{3,2,1,0:T(8,128)S(1)} %get-tuple-element.18), channel_id=1, source_target_pairs={{0,4},{4,0},{1,5},{5,1},{2,6},{6,2},{3,7},{7,3},{8,12},{12,8},{9,1... | collective-permute-start | bytes 6152 | tf_op jit(solution)/shard_map/ppermute | solution.py:14
  6.2 4.2 %collective-permute-done = f32[4,4,16,2]{3,2,1,0:T(8,128)S(1)} collective-permute-done((f32[4,4,16,2]{3,2,1,0:T(8,128)S(1)}, f32[4,4,16,2]{3,2,1,0:T(8,128)S(1)}, u32[]{:S(2)}, u32[]{:S(2)}) %collective-permute-start) | collective-permute-done | bytes 2080 | tf_op jit(solution)/shard_map/ppermute | solution.py:14
  10.4 2.0 %collective-permute-done.1 = f32[4,4,16,2]{3,2,1,0:T(8,128)S(1)} collective-permute-done((f32[4,4,16,2]{3,2,1,0:T(8,128)S(1)}, f32[4,4,16,2]{3,2,1,0:T(8,128)S(1)}, u32[]{:S(2)}, u32[]{:S(2)}) %collective-permute-start.1) | collective-permute-done | bytes 2080 | tf_op jit(solution)/shard_map/ppermute | solution.py:15
  12.6 1.3 %collective-permute-start.2 = (f32[4,4,2,132]{3,2,1,0:T(2,128)S(1)}, f32[4,4,2,132]{3,2,1,0:T(2,128)S(1)}, u32[]{:S(2)}, u32[]{:S(2)}) collective-permute-start(f32[4,4,2,132]{3,2,1,0:T(2,128)S(1)} %get-tuple-element.16), channel_id=1, source_target_pairs={{0,8},{8,16},{16,24},{1,9},{9,17},{17,25},{2,10},{10,18},{18,26},{... | collective-permute-start | bytes 50696 | tf_op jit(solution)/shard_map/ppermute | solution.py:14
  13.9 1.3 %collective-permute-start.3 = (f32[4,4,2,132]{3,2,1,0:T(2,128)S(1)}, f32[4,4,2,132]{3,2,1,0:T(2,128)S(1)}, u32[]{:S(2)}, u32[]{:S(2)}) collective-permute-start(f32[4,4,2,132]{3,2,1,0:T(2,128)S(1)} %get-tuple-element.17), channel_id=1, source_target_pairs={{8,0},{16,8},{24,16},{9,1},{17,9},{25,17},{10,2},{18,10},{26,18},{... | collective-permute-start | bytes 50696 | tf_op jit(solution)/shard_map/ppermute | solution.py:15
  15.2 3.7 %collective-permute-done.3 = f32[4,4,2,132]{3,2,1,0:T(2,128)S(1)} collective-permute-done((f32[4,4,2,132]{3,2,1,0:T(2,128)S(1)}, f32[4,4,2,132]{3,2,1,0:T(2,128)S(1)}, u32[]{:S(2)}, u32[]{:S(2)}) %collective-permute-start.3) | collective-permute-done | bytes 16928 | tf_op jit(solution)/shard_map/ppermute | solution.py:15
  19.2 3.5 %collective-permute-start.4 = (f32[4,2,20,132]{3,2,1,0:T(8,128)S(1)}, f32[4,2,20,132]{3,2,1,0:T(8,128)S(1)}, u32[]{:S(2)}, u32[]{:S(2)}) collective-permute-start(f32[4,2,20,132]{3,2,1,0:T(8,128)S(1)} %get-tuple-element.14), channel_id=1, source_target_pairs={{0,1},{1,2},{2,3},{4,5},{5,6},{6,7},{8,9},{9,10},{10,11},{12,13},{... | collective-permute-start | bytes 253448 | tf_op jit(solution)/shard_map/ppermute | solution.py:14
  22.7 1.3 %collective-permute-start.5 = (f32[4,2,20,132]{3,2,1,0:T(8,128)S(1)}, f32[4,2,20,132]{3,2,1,0:T(8,128)S(1)}, u32[]{:S(2)}, u32[]{:S(2)}) collective-permute-start(f32[4,2,20,132]{3,2,1,0:T(8,128)S(1)} %get-tuple-element.15), channel_id=1, source_target_pairs={{1,0},{2,1},{3,2},{5,4},{6,5},{7,6},{9,8},{10,9},{11,10},{13,12},{... | collective-permute-start | bytes 253448 | tf_op jit(solution)/shard_map/ppermute | solution.py:15
  24.0 2.3 %collective-permute-done.4 = f32[4,2,20,132]{3,2,1,0:T(8,128)S(1)} collective-permute-done((f32[4,2,20,132]{3,2,1,0:T(8,128)S(1)}, f32[4,2,20,132]{3,2,1,0:T(8,128)S(1)}, u32[]{:S(2)}, u32[]{:S(2)}) %collective-permute-start.4) | collective-permute-done | bytes 84512 | tf_op jit(solution)/shard_map/ppermute | solution.py:14
  26.3 4.7 %collective-permute-done.5 = f32[4,2,20,132]{3,2,1,0:T(8,128)S(1)} collective-permute-done((f32[4,2,20,132]{3,2,1,0:T(8,128)S(1)}, f32[4,2,20,132]{3,2,1,0:T(8,128)S(1)}, u32[]{:S(2)}, u32[]{:S(2)}) %collective-permute-start.5) | collective-permute-done | bytes 84512 | tf_op jit(solution)/shard_map/ppermute | solution.py:15
  32.1 11.8 %gather_fusion = f32[2048]{0:T(1024)S(1)} fusion(f32[8192]{0:T(1024)S(1)} %bitcast.24, s32[2048]{0:T(1024)S(1)} %get-tuple-element.3), kind=kCustom, calls=%fused_computation | custom fusion | bytes 24576 | tf_op jit(solution)/shard_map/gather | solution.py:88
  43.9 11.3 %scatter_custom_fusion = f32[8192]{0:T(1024)S(1)} fusion(s32[2048]{0:T(1024)S(1)} %get-tuple-element.4, f32[2048]{0:T(1024)S(1)} %subtract_select_fusion, f32[]{:T(128)} %constant.16.clone.1), kind=kCustom, calls=%fused_computation.107 | custom fusion | flops 2048 | bytes 32772 | tf_op jit(solution)/shard_map/scatter-add | solution.py:90
  55.2 1.5 %collective-permute-start.6 = (f32[1,4,16,2]{3,2,1,0:T(8,128)S(1)}, f32[1,4,16,2]{3,2,1,0:T(8,128)S(1)}, u32[]{:S(2)}, u32[]{:S(2)}) collective-permute-start(f32[1,4,16,2]{3,2,1,0:T(8,128)S(1)} %get-tuple-element.24), channel_id=1, source_target_pairs={{0,4},{4,0},{1,5},{5,1},{2,6},{6,2},{3,7},{7,3},{8,12},{12,8},{9,1... | collective-permute-start | bytes 1544 | tf_op jit(solution)/shard_map/ppermute | solution.py:14
  57.4 1.9 %collective-permute-done.6 = f32[1,4,16,2]{3,2,1,0:T(8,128)S(1)} collective-permute-done((f32[1,4,16,2]{3,2,1,0:T(8,128)S(1)}, f32[1,4,16,2]{3,2,1,0:T(8,128)S(1)}, u32[]{:S(2)}, u32[]{:S(2)}) %collective-permute-start.6) | collective-permute-done | bytes 544 | tf_op jit(solution)/shard_map/ppermute | solution.py:14
  59.3 1.7 %collective-permute-done.7 = f32[1,4,16,2]{3,2,1,0:T(8,128)S(1)} collective-permute-done((f32[1,4,16,2]{3,2,1,0:T(8,128)S(1)}, f32[1,4,16,2]{3,2,1,0:T(8,128)S(1)}, u32[]{:S(2)}, u32[]{:S(2)}) %collective-permute-start.7) | collective-permute-done | bytes 544 | tf_op jit(solution)/shard_map/ppermute | solution.py:15
  61.1 2.0 %collective-permute-start.8 = (f32[1,4,2,132]{3,2,1,0:T(2,128)S(1)}, f32[1,4,2,132]{3,2,1,0:T(2,128)S(1)}, u32[]{:S(2)}, u32[]{:S(2)}) collective-permute-start(f32[1,4,2,132]{3,2,1,0:T(2,128)S(1)} %get-tuple-element.22), channel_id=1, source_target_pairs={{0,8},{8,16},{16,24},{1,9},{9,17},{17,25},{2,10},{10,18},{18,26},{... | collective-permute-start | bytes 12680 | tf_op jit(solution)/shard_map/ppermute | solution.py:14
  63.1 1.3 %collective-permute-start.9 = (f32[1,4,2,132]{3,2,1,0:T(2,128)S(1)}, f32[1,4,2,132]{3,2,1,0:T(2,128)S(1)}, u32[]{:S(2)}, u32[]{:S(2)}) collective-permute-start(f32[1,4,2,132]{3,2,1,0:T(2,128)S(1)} %get-tuple-element.23), channel_id=1, source_target_pairs={{8,0},{16,8},{24,16},{9,1},{17,9},{25,17},{10,2},{18,10},{26,18},{... | collective-permute-start | bytes 12680 | tf_op jit(solution)/shard_map/ppermute | solution.py:15
  64.6 2.6 %collective-permute-done.9 = f32[1,4,2,132]{3,2,1,0:T(2,128)S(1)} collective-permute-done((f32[1,4,2,132]{3,2,1,0:T(2,128)S(1)}, f32[1,4,2,132]{3,2,1,0:T(2,128)S(1)}, u32[]{:S(2)}, u32[]{:S(2)}) %collective-permute-start.9) | collective-permute-done | bytes 4256 | tf_op jit(solution)/shard_map/ppermute | solution.py:15
  67.3 3.5 %collective-permute-start.10 = (f32[1,2,20,132]{3,2,1,0:T(8,128)S(1)}, f32[1,2,20,132]{3,2,1,0:T(8,128)S(1)}, u32[]{:S(2)}, u32[]{:S(2)}) collective-permute-start(f32[1,2,20,132]{3,2,1,0:T(8,128)S(1)} %get-tuple-element.20), channel_id=1, source_target_pairs={{0,1},{1,2},{2,3},{4,5},{5,6},{6,7},{8,9},{9,10},{10,11},{12,13},{... | collective-permute-start | bytes 63368 | tf_op jit(solution)/shard_map/ppermute | solution.py:14
  70.8 1.3 %collective-permute-start.11 = (f32[1,2,20,132]{3,2,1,0:T(8,128)S(1)}, f32[1,2,20,132]{3,2,1,0:T(8,128)S(1)}, u32[]{:S(2)}, u32[]{:S(2)}) collective-permute-start(f32[1,2,20,132]{3,2,1,0:T(8,128)S(1)} %get-tuple-element.21), channel_id=1, source_target_pairs={{1,0},{2,1},{3,2},{5,4},{6,5},{7,6},{9,8},{10,9},{11,10},{13,12},{... | collective-permute-start | bytes 63368 | tf_op jit(solution)/shard_map/ppermute | solution.py:15
  72.5 4.3 %collective-permute-done.11 = f32[1,2,20,132]{3,2,1,0:T(8,128)S(1)} collective-permute-done((f32[1,2,20,132]{3,2,1,0:T(8,128)S(1)}, f32[1,2,20,132]{3,2,1,0:T(8,128)S(1)}, u32[]{:S(2)}, u32[]{:S(2)}) %collective-permute-start.11) | collective-permute-done | bytes 21152 | tf_op jit(solution)/shard_map/ppermute | solution.py:15
  79.2 0.8 subtract_convert_fusion
  (49 shorter events, 5.8 us)
Async XLA Ops:
  2.1 0.8 %copy-start.2 = (bf16[3,4,16,128]{3,2,1,0:T(8,128)(2,1)S(1)}, bf16[3,4,16,128]{3,2,1,0:T(8,128)(2,1)}, u32[]{:S(2)}) copy-start(bf16[3,4,16,128]{3,2,1,0:T(8,128)(2,1)} %param.6) | copy-start | bytes 147460
  2.9 3.3 %copy-start.5 = (s32[2048]{0:T(1024)S(1)}, s32[2048]{0:T(1024)}, u32[]{:S(2)}) copy-start(s32[2048]{0:T(1024)} %param.7) | copy-start | bytes 24580
  3.0 3.2 %copy-start.4 = (s32[2048]{0:T(1024)S(1)}, s32[2048]{0:T(1024)}, u32[]{:S(2)}) copy-start(s32[2048]{0:T(1024)} %param.8) | copy-start | bytes 24580
  3.0 7.4 %collective-permute-start = (f32[4,4,16,2]{3,2,1,0:T(8,128)S(1)}, f32[4,4,16,2]{3,2,1,0:T(8,128)S(1)}, u32[]{:S(2)}, u32[]{:S(2)}) collective-permute-start(f32[4,4,16,2]{3,2,1,0:T(8,128)S(1)} %get-tuple-element.18), channel_id=1, source_target_pairs={{0,4},{4,0},{1,5},{5,1},{2,6},{6,2},{3,7},{7,3},{8,12},{12,8},{9,1... | collective-permute-start | bytes 6152 | tf_op jit(solution)/shard_map/ppermute | solution.py:14
  6.1 6.3 %collective-permute-start.1 = (f32[4,4,16,2]{3,2,1,0:T(8,128)S(1)}, f32[4,4,16,2]{3,2,1,0:T(8,128)S(1)}, u32[]{:S(2)}, u32[]{:S(2)}) collective-permute-start(f32[4,4,16,2]{3,2,1,0:T(8,128)S(1)} %get-tuple-element.19), channel_id=1, source_target_pairs={{4,0},{0,4},{5,1},{1,5},{6,2},{2,6},{7,3},{3,7},{12,8},{8,12},{13,... | collective-permute-start | bytes 6152 | tf_op jit(solution)/shard_map/ppermute | solution.py:15
  12.6 2.6 %collective-permute-start.2 = (f32[4,4,2,132]{3,2,1,0:T(2,128)S(1)}, f32[4,4,2,132]{3,2,1,0:T(2,128)S(1)}, u32[]{:S(2)}, u32[]{:S(2)}) collective-permute-start(f32[4,4,2,132]{3,2,1,0:T(2,128)S(1)} %get-tuple-element.16), channel_id=1, source_target_pairs={{0,8},{8,16},{16,24},{1,9},{9,17},{17,25},{2,10},{10,18},{18,26},{... | collective-permute-start | bytes 50696 | tf_op jit(solution)/shard_map/ppermute | solution.py:14
  13.9 5.0 %collective-permute-start.3 = (f32[4,4,2,132]{3,2,1,0:T(2,128)S(1)}, f32[4,4,2,132]{3,2,1,0:T(2,128)S(1)}, u32[]{:S(2)}, u32[]{:S(2)}) collective-permute-start(f32[4,4,2,132]{3,2,1,0:T(2,128)S(1)} %get-tuple-element.17), channel_id=1, source_target_pairs={{8,0},{16,8},{24,16},{9,1},{17,9},{25,17},{10,2},{18,10},{26,18},{... | collective-permute-start | bytes 50696 | tf_op jit(solution)/shard_map/ppermute | solution.py:15
  19.2 7.1 %collective-permute-start.4 = (f32[4,2,20,132]{3,2,1,0:T(8,128)S(1)}, f32[4,2,20,132]{3,2,1,0:T(8,128)S(1)}, u32[]{:S(2)}, u32[]{:S(2)}) collective-permute-start(f32[4,2,20,132]{3,2,1,0:T(8,128)S(1)} %get-tuple-element.14), channel_id=1, source_target_pairs={{0,1},{1,2},{2,3},{4,5},{5,6},{6,7},{8,9},{9,10},{10,11},{12,13},{... | collective-permute-start | bytes 253448 | tf_op jit(solution)/shard_map/ppermute | solution.py:14
  22.7 8.3 %collective-permute-start.5 = (f32[4,2,20,132]{3,2,1,0:T(8,128)S(1)}, f32[4,2,20,132]{3,2,1,0:T(8,128)S(1)}, u32[]{:S(2)}, u32[]{:S(2)}) collective-permute-start(f32[4,2,20,132]{3,2,1,0:T(8,128)S(1)} %get-tuple-element.15), channel_id=1, source_target_pairs={{1,0},{2,1},{3,2},{5,4},{6,5},{7,6},{9,8},{10,9},{11,10},{13,12},{... | collective-permute-start | bytes 253448 | tf_op jit(solution)/shard_map/ppermute | solution.py:15
  32.0 11.8 %copy-start = (f32[1,4,16,128]{3,2,1,0:T(8,128)}, f32[1,4,16,128]{3,2,1,0:T(8,128)S(1)}, u32[]{:S(2)}) copy-start(f32[1,4,16,128]{3,2,1,0:T(8,128)S(1)} %fusion.33) | copy-start | bytes 98308
  32.0 11.8 %copy-start.6 = (f32[2048]{0:T(1024)S(1)}, f32[2048]{0:T(1024)}, u32[]{:S(2)}) copy-start(f32[2048]{0:T(1024)} %param.9) | copy-start | bytes 24580
  55.2 4.1 %collective-permute-start.6 = (f32[1,4,16,2]{3,2,1,0:T(8,128)S(1)}, f32[1,4,16,2]{3,2,1,0:T(8,128)S(1)}, u32[]{:S(2)}, u32[]{:S(2)}) collective-permute-start(f32[1,4,16,2]{3,2,1,0:T(8,128)S(1)} %get-tuple-element.24), channel_id=1, source_target_pairs={{0,4},{4,0},{1,5},{5,1},{2,6},{6,2},{3,7},{7,3},{8,12},{12,8},{9,1... | collective-permute-start | bytes 1544 | tf_op jit(solution)/shard_map/ppermute | solution.py:14
  56.8 4.2 %collective-permute-start.7 = (f32[1,4,16,2]{3,2,1,0:T(8,128)S(1)}, f32[1,4,16,2]{3,2,1,0:T(8,128)S(1)}, u32[]{:S(2)}, u32[]{:S(2)}) collective-permute-start(f32[1,4,16,2]{3,2,1,0:T(8,128)S(1)} %get-tuple-element.25), channel_id=1, source_target_pairs={{4,0},{0,4},{5,1},{1,5},{6,2},{2,6},{7,3},{3,7},{12,8},{8,12},{13,... | collective-permute-start | bytes 1544 | tf_op jit(solution)/shard_map/ppermute | solution.py:15
  61.1 3.5 %collective-permute-start.8 = (f32[1,4,2,132]{3,2,1,0:T(2,128)S(1)}, f32[1,4,2,132]{3,2,1,0:T(2,128)S(1)}, u32[]{:S(2)}, u32[]{:S(2)}) collective-permute-start(f32[1,4,2,132]{3,2,1,0:T(2,128)S(1)} %get-tuple-element.22), channel_id=1, source_target_pairs={{0,8},{8,16},{16,24},{1,9},{9,17},{17,25},{2,10},{10,18},{18,26},{... | collective-permute-start | bytes 12680 | tf_op jit(solution)/shard_map/ppermute | solution.py:14
  63.1 4.1 %collective-permute-start.9 = (f32[1,4,2,132]{3,2,1,0:T(2,128)S(1)}, f32[1,4,2,132]{3,2,1,0:T(2,128)S(1)}, u32[]{:S(2)}, u32[]{:S(2)}) collective-permute-start(f32[1,4,2,132]{3,2,1,0:T(2,128)S(1)} %get-tuple-element.23), channel_id=1, source_target_pairs={{8,0},{16,8},{24,16},{9,1},{17,9},{25,17},{10,2},{18,10},{26,18},{... | collective-permute-start | bytes 12680 | tf_op jit(solution)/shard_map/ppermute | solution.py:15
  67.3 5.2 %collective-permute-start.10 = (f32[1,2,20,132]{3,2,1,0:T(8,128)S(1)}, f32[1,2,20,132]{3,2,1,0:T(8,128)S(1)}, u32[]{:S(2)}, u32[]{:S(2)}) collective-permute-start(f32[1,2,20,132]{3,2,1,0:T(8,128)S(1)} %get-tuple-element.20), channel_id=1, source_target_pairs={{0,1},{1,2},{2,3},{4,5},{5,6},{6,7},{8,9},{9,10},{10,11},{12,13},{... | collective-permute-start | bytes 63368 | tf_op jit(solution)/shard_map/ppermute | solution.py:14
  70.8 6.0 %collective-permute-start.11 = (f32[1,2,20,132]{3,2,1,0:T(8,128)S(1)}, f32[1,2,20,132]{3,2,1,0:T(8,128)S(1)}, u32[]{:S(2)}, u32[]{:S(2)}) collective-permute-start(f32[1,2,20,132]{3,2,1,0:T(8,128)S(1)} %get-tuple-element.21), channel_id=1, source_target_pairs={{1,0},{2,1},{3,2},{5,4},{6,5},{7,6},{9,8},{10,9},{11,10},{13,12},{... | collective-permute-start | bytes 63368 | tf_op jit(solution)/shard_map/ppermute | solution.py:15
  77.6 0.6 copy-start.3
  78.3 1.0 %copy-start.1 = (bf16[4,64,512]{2,1,0:T(8,128)(2,1)S(1)}, bf16[4,64,512]{2,1,0:T(8,128)(2,1)}, u32[]{:S(2)}) copy-start(bf16[4,64,512]{2,1,0:T(8,128)(2,1)} %param.5) | copy-start | bytes 786436
where the time goes:
time: 80.9 us; the launch traced here: 80 us
  waiting for transfers between devices  27.7 us (34%)
  starting transfers between devices  20.6 us (25%)
  other arithmetic  14.9 us (18%)
  local copies, waits for them, and re-layouts  14.1 us (17%)
  matrix products  1.64 us (2%)
  between operations  1 us (1%)
    ppermute x6, waiting for transfers between devices, with_halo(): after = lax.ppermute(first, axis, down)  18.9 us
    ppermute x6, starting transfers between devices, with_halo(): before = lax.ppermute(last, axis, up)  14.8 us
    gather x1, local copies, waits for them, and re-layouts, shards(): innovation = jnp.where(inside, state.reshape(-1)[flat] - obs_value, 0.0)  11.8 us
    scatter-add x1, other arithmetic, shards(): jnp.zeros((levels_held * inner_rows * inner_cols,), jnp.float32).at[flat]  11.3 us
    ppermute x6, waiting for transfers between devices, with_halo(): before = lax.ppermute(last, axis, up)  8.85 us
    ppermute x6, starting transfers between devices, with_halo(): after = lax.ppermute(first, axis, down)  5.77 us
    unnamed x14, local copies, waits for them, and re-layouts  1.81 us
  transfers between devices with their start and end apart: 12, of which 10 were waited for; matrix products, arithmetic and copies ran while one was open for 0% of the time, Pallas kernels for 0%

commit v1 on v0

v1 whole, which is shorter than its diff:
```python
import functools

import jax
import jax.numpy as jnp
from jax import lax
from jax.experimental import pallas as pl
from jax.experimental.pallas import tpu as pltpu
from jax.sharding import PartitionSpec as P

MESH = pl.DeviceIdType.MESH
ROUNDS = 4


def bf16_parts(x, count):
    parts = []
    for _ in range(count):
        part = x.astype(jnp.bfloat16).astype(jnp.float32)
        parts.append(part)
        x = x - part
    return parts


def kernel(
    ends, outer_hbm, courant_hbm, col_hbm, lvl_hbm, val_hbm,
    state_hbm, adj_hbm, next_hbm,
    outer, courant, col, lvl, val, sums, wide, nxt, state_v, adj_v,
    lev_out, lat_out, lon_out, lev_in, lat_in, lon_in,
    in_sem, out_sem, send_sem, recv_sem,
):
    n_lat, n_lon, n_lev = ends
    levels, rows, cols = state_v.shape
    flat_rows = levels * rows
    wide_cols = outer.shape[1]
    fine = wide_cols // cols
    outer_rows = outer.shape[0] // levels

    loads = [
        pltpu.make_async_copy(src, dst, in_sem.at[i])
        for i, (src, dst) in enumerate(
            ((outer_hbm, outer), (courant_hbm, courant), (col_hbm, col), (lvl_hbm, lvl), (val_hbm, val))
        )
    ]
    for load in loads:
        load.start()

    me_lat, me_lon, me_lev = (lax.axis_index(a) for a in ("lat", "lon", "lev"))
    links = (
        ("lev", me_lev + 1, me_lev < n_lev - 1),
        ("lev", me_lev - 1, me_lev > 0),
        ("lat", me_lat + 1, me_lat < n_lat - 1),
        ("lat", me_lat - 1, me_lat > 0),
        ("lon", lax.rem(me_lon + 1, n_lon), None),
        ("lon", lax.rem(me_lon + n_lon - 1, n_lon), None),
    )
    outs = {"lev": lev_out, "lat": lat_out, "lon": lon_out}
    ins = {"lev": lev_in, "lat": lat_in, "lon": lon_in}

    def guarded(exists, action):
        if exists is None:
            action()
        else:
            pl.when(exists)(action)

    barrier = pltpu.get_barrier_semaphore()
    for axis, who, exists in links:
        guarded(
            exists,
            lambda axis=axis, who=who: pl.semaphore_signal(
                barrier, inc=1, device_id={axis: who}, device_id_type=MESH
            ),
        )

    def message(turn, which):
        axis, who, _ = links[which]
        side = which % 2
        source = outs[axis].at[turn] if axis == "lon" else outs[axis].at[turn, side]
        return pltpu.make_async_remote_copy(
            src_ref=source,
            dst_ref=ins[axis].at[turn, side],
            send_sem=send_sem.at[turn, which],
            recv_sem=recv_sem.at[turn, which],
            device_id={axis: who},
            device_id_type=MESH,
        )

    def blank(ref, side):
        for turn in range(ROUNDS):
            ref[turn, side] = jnp.zeros(ref.shape[2:], jnp.float32)

    pl.when(me_lev == 0)(lambda: blank(lev_in, 0))
    pl.when(me_lev == n_lev - 1)(lambda: blank(lev_in, 1))
    pl.when(me_lat == 0)(lambda: blank(lat_in, 0))
    pl.when(me_lat == n_lat - 1)(lambda: blank(lat_in, 1))

    lane = lax.broadcasted_iota(jnp.int32, (flat_rows, cols), 1)
    flat = lax.broadcasted_iota(jnp.int32, (flat_rows, cols), 0)
    lane3 = lax.broadcasted_iota(jnp.int32, (levels, rows, cols), 2)
    row3 = lax.broadcasted_iota(jnp.int32, (levels, rows, cols), 1)

    pool = (
        lax.broadcasted_iota(jnp.int32, (wide_cols, cols), 0) // fine
        == lax.broadcasted_iota(jnp.int32, (wide_cols, cols), 1)
    ).astype(jnp.float32).astype(jnp.bfloat16)

    loads[0].wait()
    sums[...] = jnp.dot(outer[...], pool, preferred_element_type=jnp.float32)
    coarse = sums[pl.ds(0, flat_rows, stride=fine), :]
    for k in range(1, fine):
        coarse = coarse + sums[pl.ds(k, flat_rows, stride=fine), :]
    coarse = (coarse * (1.0 / (fine * fine))).reshape(levels, rows, cols)

    def send(turn, firsts, lasts):
        lev_out[turn, 0] = lasts[0][levels - 1]
        lev_out[turn, 1] = firsts[0][0]
        lat_out[turn, 0] = lasts[1][:, rows - 1, :]
        lat_out[turn, 1] = firsts[1][:, 0, :]
        for which in range(4):
            guarded(links[which][2], lambda which=which: message(turn, which).start())
        first = firsts[2].reshape(flat_rows, cols)[:, :1]
        last = lasts[2].reshape(flat_rows, cols)[:, cols - 1 :]
        spread = jnp.where(lane == flat, first, 0.0) + jnp.where(lane == flat + flat_rows, last, 0.0)
        lon_out[turn] = jnp.sum(spread, axis=0, keepdims=True)
        for which in (4, 5):
            message(turn, which).start()

    def receive(turn, firsts, lasts):
        for which in range(4):
            guarded(links[which ^ 1][2], lambda which=which: message(turn, which).wait_recv())
        below = [
            jnp.concatenate([lev_in[turn, 0][None], lasts[0][: levels - 1]], axis=0),
            jnp.where(row3 == 0, lat_in[turn, 0][:, None, :], pltpu.roll(lasts[1], 1, axis=1)),
        ]
        above = [
            jnp.concatenate([firsts[0][1:], lev_in[turn, 1][None]], axis=0),
            jnp.where(row3 == rows - 1, lat_in[turn, 1][:, None, :], pltpu.roll(firsts[1], rows - 1, axis=1)),
        ]
        for which in (4, 5):
            message(turn, which).wait_recv()
        left = jnp.sum(
            jnp.where(lane == flat + flat_rows, lon_in[turn, 0], 0.0), axis=1, keepdims=True
        ).reshape(levels, rows, 1)
        right = jnp.sum(jnp.where(lane == flat, lon_in[turn, 1], 0.0), axis=1, keepdims=True).reshape(
            levels, rows, 1
        )
        below.append(jnp.where(lane3 == 0, left, pltpu.roll(lasts[2], 1, axis=2)))
        above.append(jnp.where(lane3 == cols - 1, right, pltpu.roll(firsts[2], cols - 1, axis=2)))
        return below, above

    expected = sum(1 if e is None else e.astype(jnp.int32) for _, _, e in links)
    pl.semaphore_wait(barrier, expected)
    send(0, [coarse] * 3, [coarse] * 3)

    loads[1].wait()
    numbers = courant[...].astype(jnp.float32)
    lower = [jnp.maximum(numbers[k], 0.0) for k in range(3)]
    upper = [jnp.maximum(-numbers[k], 0.0) for k in range(3)]
    centre = 1.0 - jnp.abs(numbers[0]) - jnp.abs(numbers[1]) - jnp.abs(numbers[2])

    for load in loads[2:]:
        load.wait()
    where_row = (lvl[...] - me_lev * levels) * rows + col[...] // cols
    where_col = col[...] % cols
    parts = bf16_parts(val[...], 3)
    pieces, width = col.shape
    row_id = lax.broadcasted_iota(jnp.int32, (flat_rows, width), 0)
    col_id = lax.broadcasted_iota(jnp.int32, (cols, width), 0)
    hits = [[] for _ in range(4)]
    tables = []
    for k in range(pieces):
        match = where_row[k : k + 1] == row_id
        hits[0].append(jnp.where(match, 1.0, 0.0).astype(jnp.bfloat16))
        for i, part in enumerate(parts):
            hits[i + 1].append(jnp.where(match, part[k : k + 1], 0.0).astype(jnp.bfloat16))
        tables.append(jnp.where(where_col[k : k + 1] == col_id, 1.0, 0.0).astype(jnp.bfloat16))
    left_side = jnp.concatenate([jnp.concatenate(h, axis=1) for h in hits], axis=0)
    totals = lax.dot_general(
        left_side, jnp.concatenate(tables, axis=1), (((1,), (1,)), ((), ())),
        preferred_element_type=jnp.float32,
    )
    count = totals[:flat_rows].reshape(levels, rows, cols)
    observed = (
        totals[flat_rows : 2 * flat_rows]
        + totals[2 * flat_rows : 3 * flat_rows]
        + totals[3 * flat_rows :]
    ).reshape(levels, rows, cols)

    def forward(field, turn):
        below, above = receive(turn, [field] * 3, [field] * 3)
        result = centre * field
        for k in range(3):
            result = result + lower[k] * below[k] + upper[k] * above[k]
        return result

    state = forward(coarse, 0)
    send(1, [state] * 3, [state] * 3)
    state = forward(state, 1)
    field = count * state - observed

    for turn in (2, 3):
        firsts = [lower[k] * field for k in range(3)]
        lasts = [upper[k] * field for k in range(3)]
        send(turn, firsts, lasts)
        if turn == 2:
            state_v[...] = state
            store_state = pltpu.make_async_copy(state_v, state_hbm, out_sem.at[0])
            store_state.start()
        below, above = receive(turn, firsts, lasts)
        result = centre * field
        for k in range(3):
            result = result + above[k] + below[k]
        field = result
    adj_v[...] = field
    store_adj = pltpu.make_async_copy(adj_v, adj_hbm, out_sem.at[1])
    store_adj.start()

    table = (
        lax.broadcasted_iota(jnp.int32, (cols, wide_cols), 0)
        == lax.broadcasted_iota(jnp.int32, (cols, wide_cols), 1) // fine
    ).astype(jnp.float32).astype(jnp.bfloat16)
    halves = bf16_parts(field.reshape(flat_rows, cols), 2)
    spread = jnp.dot(
        jnp.concatenate([h.astype(jnp.bfloat16) for h in halves], axis=1),
        jnp.concatenate([table, table], axis=0),
        preferred_element_type=jnp.float32,
    )
    for k in range(fine):
        for c in range(fine):
            span = pl.ds(c * cols, cols)
            wide[c, pl.ds(k, flat_rows, stride=fine), :] = spread[:, c * cols : (c + 1) * cols]
    stores = []
    for level in range(levels):
        span = pl.ds(level * outer_rows, outer_rows)
        for c in range(fine):
            lanes = pl.ds(c * cols, cols)
            nxt[span, lanes] = (outer[span, lanes].astype(jnp.float32) - wide[c, span, :]).astype(jnp.bfloat16)
        store = pltpu.make_async_copy(nxt.at[span], next_hbm.at[span], out_sem.at[2 + level])
        store.start()
        stores.append(store)

    for turn in range(ROUNDS):
        for which in range(6):
            guarded(links[which][2], lambda turn=turn, which=which: message(turn, which).wait_send())
    for store in [store_state, store_adj] + stores:
        store.wait()


def shards(ends, outer_increment, courant, obs_column, obs_level, obs_value):
    levels, outer_rows, wide_cols = outer_increment.shape
    _, _, rows, cols = courant.shape
    flat_rows = levels * rows
    fine = wide_cols // cols
    lanes = 128
    observed = (obs_column.shape[0] // lanes, lanes)
    assert 2 * flat_rows <= cols
    f32, bf16 = jnp.float32, jnp.bfloat16
    state, adjoint, following = pl.pallas_call(
        functools.partial(kernel, ends),
        out_shape=(
            jax.ShapeDtypeStruct((levels, rows, cols), f32),
            jax.ShapeDtypeStruct((levels, rows, cols), f32),
            jax.ShapeDtypeStruct((levels * outer_rows, wide_cols), bf16),
        ),
        in_specs=[pl.BlockSpec(memory_space=pl.ANY)] * 5,
        out_specs=(pl.BlockSpec(memory_space=pl.ANY),) * 3,
        scratch_shapes=[
            pltpu.VMEM((levels * outer_rows, wide_cols), bf16),
            pltpu.VMEM(courant.shape, bf16),
            pltpu.VMEM(observed, jnp.int32),
            pltpu.VMEM(observed, jnp.int32),
            pltpu.VMEM(observed, f32),
            pltpu.VMEM((levels * outer_rows, cols), f32),
            pltpu.VMEM((fine, levels * outer_rows, cols), f32),
            pltpu.VMEM((levels * outer_rows, wide_cols), bf16),
            pltpu.VMEM((levels, rows, cols), f32),
            pltpu.VMEM((levels, rows, cols), f32),
            pltpu.VMEM((ROUNDS, 2, rows, cols), f32),
            pltpu.VMEM((ROUNDS, 2, levels, cols), f32),
            pltpu.VMEM((ROUNDS, 1, cols), f32),
            pltpu.VMEM((ROUNDS, 2, rows, cols), f32),
            pltpu.VMEM((ROUNDS, 2, levels, cols), f32),
            pltpu.VMEM((ROUNDS, 2, 1, cols), f32),
            pltpu.SemaphoreType.DMA((5,)),
            pltpu.SemaphoreType.DMA((2 + levels,)),
            pltpu.SemaphoreType.DMA((ROUNDS, 6)),
            pltpu.SemaphoreType.DMA((ROUNDS, 6)),
        ],
        compiler_params=pltpu.CompilerParams(collective_id=0, has_side_effects=True),
    )(
        outer_increment.reshape(levels * outer_rows, wide_cols),
        courant,
        obs_column.reshape(observed),
        obs_level.reshape(observed),
        obs_value.reshape(observed),
    )
    return state, adjoint, following.reshape(outer_increment.shape)


def solution(mesh):
    ends = tuple(mesh.shape[a] for a in ("lat", "lon", "lev"))
    block = P("lev", "lat", "lon")
    observed = P(("lat", "lon"))
    return jax.shard_map(
        functools.partial(shards, ends),
        mesh=mesh,
        in_specs=(block, P(None, "lev", "lat", "lon"), observed, observed, observed),
        out_specs=(block, block, block),
        check_vma=False,
    )
```

time: 80.9 us -> 22.4 us (0.28)
  waiting for transfers between devices: 27.7 us -> 0 us
  starting transfers between devices: 20.6 us -> 0 us
  Pallas kernels: 0 us -> 17.8 us
  other arithmetic: 14.9 us -> 0 us
  local copies, waits for them, and re-layouts: 14.1 us -> 3.67 us
  matrix products: 1.64 us -> 0 us
    ppermute x12 -> x0, waiting for transfers between devices: 27.7 us -> none  [the longest x6 18.9 us: with_halo(): after = lax.ppermute(first, axis, down)]
    ppermute x12 -> x0, starting transfers between devices: 20.6 us -> none  [the longest x6 14.8 us: with_halo(): before = lax.ppermute(last, axis, up)]
    pallas_call x0 -> x1, Pallas kernels: none -> 17.8 us  [shards(): pl.pallas_call(functools.partial(kernel, ends), out_shape=(jax.ShapeDtype...]
    gather x1 -> x0, local copies, waits for them, and re-layouts: 11.8 us -> none  [shards(): innovation = jnp.where(inside, state.reshape(-1)[flat] - obs_value, 0.0)]
    scatter-add x1 -> x0, other arithmetic: 11.3 us -> none  [shards(): jnp.zeros((levels_held * inner_rows * inner_cols,), jnp.float32).at[flat]]
    unnamed x14 -> x5, local copies, waits for them, and re-layouts: 1.81 us -> 3.67 us
    dot_general x2 -> x0, matrix products: 1.64 us -> none  [the longest x1 1.27 us: shards(): jnp.dot(outer_increment.reshape(levels_dev * rows, columns), column_table...]
  transfers between devices with their start and end apart: 12 -> 0, of which waited for: 10 -> 0; matrix products, arithmetic and copies ran while one was open for 0% -> 0% of each run, Pallas kernels for 0% -> 0%
where the time goes in v1:
time: 22.4 us; the launch traced here: 22.1 us
  Pallas kernels  17.8 us (79%)
  local copies, waits for them, and re-layouts  3.67 us (16%)
  between operations  0.65 us (3%)
    pallas_call x1, Pallas kernels, shards(): pl.pallas_call(functools.partial(kernel, ends), out_shape=(jax.ShapeDtype...  17.8 us
    unnamed x5, local copies, waits for them, and re-layouts  3.67 us

profile of v1, /device:TPU:0, one launch (start us, length us, event | category | flops | bytes accessed | tf_op | source)
XLA Modules:
  0.0 22.1 jit_solution(10546465727569597997)
XLA Ops:
  0.6 17.8 %shard_map.76 = (f32[4,16,128]{2,1,0:T(8,128)}, f32[4,16,128]{2,1,0:T(8,128)}, bf16[256,512]{1,0:T(8,128)(2,1)}) custom-call(bf16[256,512]{1,0:T(8,128)(2,1)} %bitcast.5, bf16[3,4,16,128]{3,2,1,0:T(8,128)(2,1)} %courant_hbm.1, s32[16,128]{1,0:T(8,128)} %bitcast.7, s32[16,128]{1,0:T(8,128)} %bitcast.8, f32[16,128]{1,0:T(8,128)} %bitcast.9), custom_call_target="tpu_custom_call" | custom-call | tf_op jit(solution)/shard_map/pallas_call | solution.py:256
  18.4 0.0 copy-start
  18.5 1.4 %copy.11 = f32[4,16,128]{2,1,0:T(8,128)} copy(f32[4,16,128]{2,1,0:T(8,128)} %get-tuple-element.12) | data formatting | bytes 65536
  19.8 0.0 copy-done
  19.8 0.6 %copy.12 = f32[4,16,128]{2,1,0:T(8,128)} copy(f32[4,16,128]{2,1,0:T(8,128)S(1)} %copy-done) | data formatting | bytes 65536
  20.5 1.7 %copy.13 = bf16[4,64,512]{2,1,0:T(8,128)(2,1)} copy(bf16[4,64,512]{2,1,0:T(8,128)(2,1)} %bitcast.6) | data formatting | bytes 524288
Async XLA Ops:
  18.4 1.4 %copy-start = (f32[4,16,128]{2,1,0:T(8,128)S(1)}, f32[4,16,128]{2,1,0:T(8,128)}, u32[]{:S(2)}) copy-start(f32[4,16,128]{2,1,0:T(8,128)} %get-tuple-element.13) | copy-start | bytes 98308

commit v2 on v1

--- a/solution.py
+++ b/solution.py
@@ -22,17 +22,16 @@
 
 def kernel(
     ends, outer_hbm, courant_hbm, col_hbm, lvl_hbm, val_hbm,
-    state_hbm, adj_hbm, next_hbm,
-    outer, courant, col, lvl, val, sums, wide, nxt, state_v, adj_v,
+    state_v, adj_v, outer,
+    courant, col, lvl, val, sums,
     lev_out, lat_out, lon_out, lev_in, lat_in, lon_in,
-    in_sem, out_sem, send_sem, recv_sem,
+    in_sem, send_sem, recv_sem,
 ):
     n_lat, n_lon, n_lev = ends
     levels, rows, cols = state_v.shape
     flat_rows = levels * rows
     wide_cols = outer.shape[1]
     fine = wide_cols // cols
-    outer_rows = outer.shape[0] // levels
 
     loads = [
         pltpu.make_async_copy(src, dst, in_sem.at[i])
@@ -202,16 +201,31 @@
         send(turn, firsts, lasts)
         if turn == 2:
             state_v[...] = state
-            store_state = pltpu.make_async_copy(state_v, state_hbm, out_sem.at[0])
-            store_state.start()
         below, above = receive(turn, firsts, lasts)
         result = centre * field
         for k in range(3):
             result = result + above[k] + below[k]
         field = result
     adj_v[...] = field
-    store_adj = pltpu.make_async_copy(adj_v, adj_hbm, out_sem.at[1])
-    store_adj.start()
+
+    for turn in range(ROUNDS):
+        for which in range(6):
+            guarded(links[which][2], lambda turn=turn, which=which: message(turn, which).wait_send())
+
+
+def finish(state_v, adj_v, outer, state_hbm, adj_hbm, next_hbm, wide, nxt, out_sem):
+    levels, rows, cols = state_v.shape
+    flat_rows = levels * rows
+    wide_cols = outer.shape[1]
+    fine = wide_cols // cols
+    outer_rows = outer.shape[0] // levels
+    stores = [
+        pltpu.make_async_copy(state_v, state_hbm, out_sem.at[0]),
+        pltpu.make_async_copy(adj_v, adj_hbm, out_sem.at[1]),
+    ]
+    for store in stores:
+        store.start()
+    field = adj_v[...]
 
     table = (
         lax.broadcasted_iota(jnp.int32, (cols, wide_cols), 0)
@@ -225,9 +239,7 @@
     )
     for k in range(fine):
         for c in range(fine):
-            span = pl.ds(c * cols, cols)
             wide[c, pl.ds(k, flat_rows, stride=fine), :] = spread[:, c * cols : (c + 1) * cols]
-    stores = []
     for level in range(levels):
         span = pl.ds(level * outer_rows, outer_rows)
         for c in range(fine):
@@ -236,11 +248,7 @@
         store = pltpu.make_async_copy(nxt.at[span], next_hbm.at[span], out_sem.at[2 + level])
         store.start()
         stores.append(store)
-
-    for turn in range(ROUNDS):
-        for which in range(6):
-            guarded(links[which][2], lambda turn=turn, which=which: message(turn, which).wait_send())
-    for store in [store_state, store_adj] + stores:
+    for store in stores:
         store.wait()
 
 
@@ -253,26 +261,24 @@
     observed = (obs_column.shape[0] // lanes, lanes)
     assert 2 * flat_rows <= cols
     f32, bf16 = jnp.float32, jnp.bfloat16
-    state, adjoint, following = pl.pallas_call(
+    outer_shape = (levels * outer_rows, wide_cols)
+    vmem = pl.BlockSpec(memory_space=pltpu.VMEM)
+    hbm = pl.BlockSpec(memory_space=pl.ANY)
+    held = pl.pallas_call(
         functools.partial(kernel, ends),
         out_shape=(
-            jax.ShapeDtypeStruct((levels, rows, cols), f32),
-            jax.ShapeDtypeStruct((levels, rows, cols), f32),
-            jax.ShapeDtypeStruct((levels * outer_rows, wide_cols), bf16),
+            pltpu.VMEM((levels, rows, cols), f32),
+            pltpu.VMEM((levels, rows, cols), f32),
+            pltpu.VMEM(outer_shape, bf16),
         ),
-        in_specs=[pl.BlockSpec(memory_space=pl.ANY)] * 5,
-        out_specs=(pl.BlockSpec(memory_space=pl.ANY),) * 3,
+        in_specs=[hbm] * 5,
+        out_specs=(vmem,) * 3,
         scratch_shapes=[
-            pltpu.VMEM((levels * outer_rows, wide_cols), bf16),
             pltpu.VMEM(courant.shape, bf16),
             pltpu.VMEM(observed, jnp.int32),
             pltpu.VMEM(observed, jnp.int32),
             pltpu.VMEM(observed, f32),
             pltpu.VMEM((levels * outer_rows, cols), f32),
-            pltpu.VMEM((fine, levels * outer_rows, cols), f32),
-            pltpu.VMEM((levels * outer_rows, wide_cols), bf16),
-            pltpu.VMEM((levels, rows, cols), f32),
-            pltpu.VMEM((levels, rows, cols), f32),
             pltpu.VMEM((ROUNDS, 2, rows, cols), f32),
             pltpu.VMEM((ROUNDS, 2, levels, cols), f32),
             pltpu.VMEM((ROUNDS, 1, cols), f32),
@@ -280,18 +286,32 @@
             pltpu.VMEM((ROUNDS, 2, levels, cols), f32),
             pltpu.VMEM((ROUNDS, 2, 1, cols), f32),
             pltpu.SemaphoreType.DMA((5,)),
-            pltpu.SemaphoreType.DMA((2 + levels,)),
             pltpu.SemaphoreType.DMA((ROUNDS, 6)),
             pltpu.SemaphoreType.DMA((ROUNDS, 6)),
         ],
         compiler_params=pltpu.CompilerParams(collective_id=0, has_side_effects=True),
     )(
-        outer_increment.reshape(levels * outer_rows, wide_cols),
+        outer_increment.reshape(outer_shape),
         courant,
         obs_column.reshape(observed),
         obs_level.reshape(observed),
         obs_value.reshape(observed),
     )
+    state, adjoint, following = pl.pallas_call(
+        finish,
+        out_shape=(
+            jax.ShapeDtypeStruct((levels, rows, cols), f32),
+            jax.ShapeDtypeStruct((levels, rows, cols), f32),
+            jax.ShapeDtypeStruct(outer_shape, bf16),
+        ),
+        in_specs=[vmem] * 3,
+        out_specs=(hbm,) * 3,
+        scratch_shapes=[
+            pltpu.VMEM((fine, levels * outer_rows, cols), f32),
+            pltpu.VMEM(outer_shape, bf16),
+            pltpu.SemaphoreType.DMA((2 + levels,)),
+        ],
+    )(*[pltpu.with_memory_space_constraint(x, pltpu.VMEM) for x in held])
     return state, adjoint, following.reshape(outer_increment.shape)
 
 

time: 22.4 us -> 18.6 us (0.83)
  local copies, waits for them, and re-layouts: 3.67 us -> 0 us
    unnamed x5 -> x0, local copies, waits for them, and re-layouts: 3.67 us -> none
    pallas_call x1 -> x2, Pallas kernels: 17.8 us -> 17.8 us  [the longest x1 16.8 us: shards(): pl.pallas_call(functools.partial(kernel, ends), out_shape=(pltpu.VMEM((le...]
where the time goes in v2:
time: 18.6 us; the launch traced here: 18.4 us
  Pallas kernels  17.8 us (96%)
  between operations  0.64 us (3%)
    pallas_call x1, Pallas kernels, shards(): pl.pallas_call(functools.partial(kernel, ends), out_shape=(pltpu.VMEM((le...  16.8 us
    pallas_call x1, Pallas kernels, shards(): pl.pallas_call(finish, out_shape=(jax.ShapeDtypeStruct((levels, rows, col...  0.94 us

profile of v2, /device:TPU:0, one launch (start us, length us, event | category | flops | bytes accessed | tf_op | source)
XLA Modules:
  0.0 18.4 jit_solution(11944022914575901600)
XLA Ops:
  0.6 16.8 %shard_map.76 = (f32[4,16,128]{2,1,0:T(8,128)S(1)}, f32[4,16,128]{2,1,0:T(8,128)S(1)}, bf16[256,512]{1,0:T(8,128)(2,1)S(1)}) custom-call(bf16[256,512]{1,0:T(8,128)(2,1)} %bitcast.5, bf16[3,4,16,128]{3,2,1,0:T(8,128)(2,1)} %courant_hbm.1, s32[16,128]{1,0:T(8,128)} %bitcast.6, s32[16,128]{1,0:T(8,128)} %bitcast.7, f32[16,128]{1,0:T(8,128)} %bitcast.8), custom_call_target="tpu_custom_call" | custom-call | tf_op jit(solution)/shard_map/pallas_call | solution.py:267
  17.5 0.9 %shard_map.77 = (f32[4,16,128]{2,1,0:T(8,128)}, f32[4,16,128]{2,1,0:T(8,128)}, bf16[256,512]{1,0:T(8,128)(2,1)}) custom-call(f32[4,16,128]{2,1,0:T(8,128)S(1)} %get-tuple-element.9.state_v, f32[4,16,128]{2,1,0:T(8,128)S(1)} %get-tuple-element.10.adj_v, bf16[256,512]{1,0:T(8,128)(2,1)S(1)} %get-tuple-element.11.outer), custom_call_target="tpu_custom_call" | custom-call | tf_op jit(solution)/shard_map/pallas_call | solution.py:300

commit v3 on v2

--- a/solution.py
+++ b/solution.py
@@ -8,7 +8,7 @@
 from jax.sharding import PartitionSpec as P
 
 MESH = pl.DeviceIdType.MESH
-ROUNDS = 4
+ROUNDS = 3
 
 
 def bf16_parts(x, count):
@@ -25,7 +25,8 @@
     state_v, adj_v, outer,
     courant, col, lvl, val, sums,
     lev_out, lat_out, lon_out, lev_in, lat_in, lon_in,
-    in_sem, send_sem, recv_sem,
+    lev2_out, lat2_out, edge_out, pack_out, lev2_in, lat2_in, edge_in, pack_in,
+    in_sem, send_sem, recv_sem, send2_sem, recv2_sem,
 ):
     n_lat, n_lon, n_lev = ends
     levels, rows, cols = state_v.shape
@@ -51,6 +52,36 @@
         ("lon", lax.rem(me_lon + 1, n_lon), None),
         ("lon", lax.rem(me_lon + n_lon - 1, n_lon), None),
     )
+    side_lev = (links[0], links[1])
+    side_lat = (links[2], links[3])
+    side_lon = (links[4], links[5])
+
+    def joined(*sides):
+        exists = [e for _, _, e in sides if e is not None]
+        target = {axis: who for axis, who, _ in sides}
+        return target, functools.reduce(jnp.logical_and, exists) if exists else None
+
+    wide_links = []
+
+    def add(sides, opposite, source, landing):
+        target, exists = joined(*sides)
+        wide_links.append((target, exists, joined(*opposite)[1], source, landing))
+
+    for s in range(2):
+        add([side_lev[s]], [side_lev[1 - s]], lev2_out.at[s], lev2_in.at[s])
+        add([side_lat[s]], [side_lat[1 - s]], lat2_out.at[s], lat2_in.at[s])
+    for s in range(2):
+        for t in range(2):
+            add([side_lev[s], side_lat[t]], [side_lev[1 - s], side_lat[1 - t]],
+                edge_out.at[2 * s + t], edge_in.at[2 * s + t])
+    faces_end = len(wide_links)
+    for u in range(2):
+        add([side_lon[u]], [side_lon[1 - u]], pack_out, pack_in.at[u])
+    for base, sides in ((2, side_lev), (6, side_lat)):
+        for s in range(2):
+            for u in range(2):
+                add([sides[s], side_lon[u]], [sides[1 - s], side_lon[1 - u]],
+                    pack_out, pack_in.at[base + 2 * s + u])
     outs = {"lev": lev_out, "lat": lat_out, "lon": lon_out}
     ins = {"lev": lev_in, "lat": lat_in, "lon": lon_in}
 
@@ -61,13 +92,31 @@
             pl.when(exists)(action)
 
     barrier = pltpu.get_barrier_semaphore()
-    for axis, who, exists in links:
+    for target, exists, _, _, _ in wide_links:
         guarded(
             exists,
-            lambda axis=axis, who=who: pl.semaphore_signal(
-                barrier, inc=1, device_id={axis: who}, device_id_type=MESH
+            lambda target=target: pl.semaphore_signal(
+                barrier, inc=1, device_id=target, device_id_type=MESH
             ),
         )
+
+    def wide_message(i):
+        target, _, _, source, landing = wide_links[i]
+        return pltpu.make_async_remote_copy(
+            src_ref=source,
+            dst_ref=landing,
+            send_sem=send2_sem.at[i],
+            recv_sem=recv2_sem.at[i],
+            device_id=target,
+            device_id_type=MESH,
+        )
+
+    def clear(landing):
+        landing[...] = jnp.zeros(landing.shape, jnp.float32)
+
+    for _, _, arrives, _, landing in wide_links:
+        if arrives is not None:
+            pl.when(jnp.logical_not(arrives))(lambda landing=landing: clear(landing))
 
     def message(turn, which):
         axis, who, _ = links[which]
@@ -108,6 +157,37 @@
         coarse = coarse + sums[pl.ds(k, flat_rows, stride=fine), :]
     coarse = (coarse * (1.0 / (fine * fine))).reshape(levels, rows, cols)
 
+    def pack(first, last):
+        first = first.reshape(flat_rows, cols)[:, :1]
+        last = last.reshape(flat_rows, cols)[:, cols - 1 :]
+        spread = jnp.where(lane == flat, first, 0.0) + jnp.where(lane == flat + flat_rows, last, 0.0)
+        return jnp.sum(spread, axis=0, keepdims=True)
+
+    def column(row, begin, step, length):
+        at = lax.broadcasted_iota(jnp.int32, (length, cols), 1)
+        index = lax.broadcasted_iota(jnp.int32, (length, cols), 0)
+        return jnp.sum(jnp.where(at == begin + step * index, row, 0.0), axis=1, keepdims=True)
+
+    def either(from_previous, from_next):
+        at = lax.broadcasted_iota(jnp.int32, from_next.shape, 1)
+        return jnp.where(at < flat_rows, from_next, from_previous)
+
+    def ends_of(row):
+        return [column(row, b, 1, flat_rows).reshape(levels, rows, 1) for b in (flat_rows, 0)]
+
+    def shifted(firsts, lasts, lev, lat, lon):
+        below = [
+            jnp.concatenate([lev[0][None], lasts[0][: levels - 1]], axis=0),
+            jnp.where(row3 == 0, lat[0][:, None, :], pltpu.roll(lasts[1], 1, axis=1)),
+            jnp.where(lane3 == 0, lon[0], pltpu.roll(lasts[2], 1, axis=2)),
+        ]
+        above = [
+            jnp.concatenate([firsts[0][1:], lev[1][None]], axis=0),
+            jnp.where(row3 == rows - 1, lat[1][:, None, :], pltpu.roll(firsts[1], rows - 1, axis=1)),
+            jnp.where(lane3 == cols - 1, lon[1], pltpu.roll(firsts[2], cols - 1, axis=2)),
+        ]
+        return below, above
+
     def send(turn, firsts, lasts):
         lev_out[turn, 0] = lasts[0][levels - 1]
         lev_out[turn, 1] = firsts[0][0]
@@ -115,37 +195,20 @@
         lat_out[turn, 1] = firsts[1][:, 0, :]
         for which in range(4):
             guarded(links[which][2], lambda which=which: message(turn, which).start())
-        first = firsts[2].reshape(flat_rows, cols)[:, :1]
-        last = lasts[2].reshape(flat_rows, cols)[:, cols - 1 :]
-        spread = jnp.where(lane == flat, first, 0.0) + jnp.where(lane == flat + flat_rows, last, 0.0)
-        lon_out[turn] = jnp.sum(spread, axis=0, keepdims=True)
+        lon_out[turn] = pack(firsts[2], lasts[2])
         for which in (4, 5):
             message(turn, which).start()
 
-    def receive(turn, firsts, lasts):
-        for which in range(4):
+    def receive(turn):
+        for which in range(6):
             guarded(links[which ^ 1][2], lambda which=which: message(turn, which).wait_recv())
-        below = [
-            jnp.concatenate([lev_in[turn, 0][None], lasts[0][: levels - 1]], axis=0),
-            jnp.where(row3 == 0, lat_in[turn, 0][:, None, :], pltpu.roll(lasts[1], 1, axis=1)),
-        ]
-        above = [
-            jnp.concatenate([firsts[0][1:], lev_in[turn, 1][None]], axis=0),
-            jnp.where(row3 == rows - 1, lat_in[turn, 1][:, None, :], pltpu.roll(firsts[1], rows - 1, axis=1)),
-        ]
-        for which in (4, 5):
-            message(turn, which).wait_recv()
-        left = jnp.sum(
-            jnp.where(lane == flat + flat_rows, lon_in[turn, 0], 0.0), axis=1, keepdims=True
-        ).reshape(levels, rows, 1)
-        right = jnp.sum(jnp.where(lane == flat, lon_in[turn, 1], 0.0), axis=1, keepdims=True).reshape(
-            levels, rows, 1
+        return (
+            [lev_in[turn, 0], lev_in[turn, 1]],
+            [lat_in[turn, 0], lat_in[turn, 1]],
+            either(lon_in[turn, 0], lon_in[turn, 1]),
         )
-        below.append(jnp.where(lane3 == 0, left, pltpu.roll(lasts[2], 1, axis=2)))
-        above.append(jnp.where(lane3 == cols - 1, right, pltpu.roll(firsts[2], cols - 1, axis=2)))
-        return below, above
-
-    expected = sum(1 if e is None else e.astype(jnp.int32) for _, _, e in links)
+
+    expected = sum(1 if link[1] is None else link[1].astype(jnp.int32) for link in wide_links)
     pl.semaphore_wait(barrier, expected)
     send(0, [coarse] * 3, [coarse] * 3)
 
@@ -154,6 +217,8 @@
     lower = [jnp.maximum(numbers[k], 0.0) for k in range(3)]
     upper = [jnp.maximum(-numbers[k], 0.0) for k in range(3)]
     centre = 1.0 - jnp.abs(numbers[0]) - jnp.abs(numbers[1]) - jnp.abs(numbers[2])
+
+    send(2, lower, upper)
 
     for load in loads[2:]:
         load.wait()
@@ -184,7 +249,8 @@
     ).reshape(levels, rows, cols)
 
     def forward(field, turn):
-        below, above = receive(turn, [field] * 3, [field] * 3)
+        lev, lat, lon = receive(turn)
+        below, above = shifted([field] * 3, [field] * 3, lev, lat, ends_of(lon))
         result = centre * field
         for k in range(3):
             result = result + lower[k] * below[k] + upper[k] * above[k]
@@ -195,22 +261,106 @@
     state = forward(state, 1)
     field = count * state - observed
 
-    for turn in (2, 3):
-        firsts = [lower[k] * field for k in range(3)]
-        lasts = [upper[k] * field for k in range(3)]
-        send(turn, firsts, lasts)
-        if turn == 2:
-            state_v[...] = state
-        below, above = receive(turn, firsts, lasts)
-        result = centre * field
-        for k in range(3):
-            result = result + above[k] + below[k]
-        field = result
+    state_v[...] = state
+    lev3 = lax.broadcasted_iota(jnp.int32, (levels, rows, cols), 0)
+    to_first = [lower[k] * field for k in range(3)]
+    to_last = [upper[k] * field for k in range(3)]
+    none_lev = jnp.zeros((rows, cols), jnp.float32)
+    none_lat = jnp.zeros((levels, cols), jnp.float32)
+    below, above = shifted(to_first, to_last, [none_lev] * 2, [none_lat] * 2, [0.0, 0.0])
+    partial = centre * field
+    for k in range(3):
+        partial = partial + above[k] + below[k]
+
+    last_lev, last_row = levels - 1, rows - 1
+    lev_edge = (last_lev, 0)
+    row_edge = (last_row, 0)
+    for s in range(2):
+        lev_move = (to_last, to_first)[s]
+        lev2_out[s, 0] = partial[lev_edge[s]]
+        lev2_out[s, 1] = lev_move[0][lev_edge[s]]
+        lat2_out[s, 0] = partial[:, row_edge[s], :]
+        lat2_out[s, 1] = lev_move[1][:, row_edge[s], :]
+        for t in range(2):
+            lat_move = (to_last, to_first)[t]
+            r = row_edge[t]
+            edge_out[2 * s + t, 0:1] = lat_move[1][lev_edge[s], r : r + 1, :]
+            edge_out[2 * s + t, 1:2] = lev_move[0][lev_edge[s], r : r + 1, :]
+    for i in range(faces_end):
+        guarded(wide_links[i][1], lambda i=i: wide_message(i).start())
+    moved_lon = pack(to_first[2], to_last[2])
+    at_lev_ends = jnp.where(lev3 == 0, to_first[0], jnp.where(lev3 == last_lev, to_last[0], 0.0))
+    at_row_ends = jnp.where(row3 == 0, to_first[1], jnp.where(row3 == last_row, to_last[1], 0.0))
+    pack_out[0:1] = pack(partial, partial)
+    pack_out[1:2] = moved_lon
+    pack_out[2:3] = pack(at_lev_ends, at_lev_ends)
+    pack_out[3:4] = pack(at_row_ends, at_row_ends)
+    for i in range(faces_end, len(wide_links)):
+        guarded(wide_links[i][1], lambda i=i: wide_message(i).start())
+
+    speed_lev, speed_lat, speed_lon = receive(2)
+    for i in range(len(wide_links)):
+        guarded(wide_links[i][2], lambda i=i: wide_message(i).wait_recv())
+    side_pack = either(pack_in[0], pack_in[1])
+    lev_pack = [either(pack_in[2 + 2 * s], pack_in[3 + 2 * s]) for s in range(2)]
+    lat_pack = [either(pack_in[6 + 2 * s], pack_in[7 + 2 * s]) for s in range(2)]
+
+    left, right = ends_of(side_pack[1:2])
+    field = partial + jnp.where(lane3 == 0, left, 0.0) + jnp.where(lane3 == cols - 1, right, 0.0)
+    field = field + jnp.where(lev3 == 0, lev2_in[0, 1][None], 0.0)
+    field = field + jnp.where(lev3 == last_lev, lev2_in[1, 1][None], 0.0)
+    field = field + jnp.where(row3 == 0, lat2_in[0, 1][:, None, :], 0.0)
+    field = field + jnp.where(row3 == last_row, lat2_in[1, 1][:, None, :], 0.0)
+
+    plane_row = lax.broadcasted_iota(jnp.int32, (rows, cols), 0)
+    plane_lane = lax.broadcasted_iota(jnp.int32, (rows, cols), 1)
+    line_lev = lax.broadcasted_iota(jnp.int32, (levels, cols), 0)
+    line_lane = lax.broadcasted_iota(jnp.int32, (levels, cols), 1)
+    beside_lev, beside_lat = [], []
+    for s in range(2):
+        own = (to_first[0][0], to_last[0][last_lev])[s]
+        plane = lev2_in[s, 0] + own
+        plane = plane + jnp.where(plane_row == 0, edge_in[2 * s, 0:1], 0.0)
+        plane = plane + jnp.where(plane_row == last_row, edge_in[2 * s + 1, 0:1], 0.0)
+        begin = lev_edge[s] * rows
+        moved = lev_pack[s][1:2]
+        plane = plane + jnp.where(plane_lane == 0, column(moved, flat_rows + begin, 1, rows), 0.0)
+        plane = plane + jnp.where(plane_lane == cols - 1, column(moved, begin, 1, rows), 0.0)
+        beside_lev.append(plane * speed_lev[s])
+
+        own = (to_first[1][:, 0, :], to_last[1][:, last_row, :])[s]
+        plane = lat2_in[s, 0] + own
+        plane = plane + jnp.where(line_lev == 0, edge_in[s, 1:2], 0.0)
+        plane = plane + jnp.where(line_lev == last_lev, edge_in[2 + s, 1:2], 0.0)
+        begin = row_edge[s]
+        moved = lat_pack[s][1:2]
+        plane = plane + jnp.where(line_lane == 0, column(moved, flat_rows + begin, rows, levels), 0.0)
+        plane = plane + jnp.where(line_lane == cols - 1, column(moved, begin, rows, levels), 0.0)
+        beside_lat.append(plane * speed_lat[s])
+    at = lax.rem(lax.broadcasted_iota(jnp.int32, (1, cols), 1), flat_rows)
+    at_lev, at_row = lax.div(at, rows), lax.rem(at, rows)
+    ring = side_pack[0:1] + pltpu.roll(moved_lon, flat_rows, axis=1)
+    ring = ring + jnp.where(at_lev == 0, pltpu.roll(lev_pack[0][2:3], cols - last_lev * rows, axis=1), 0.0)
+    ring = ring + jnp.where(at_lev == last_lev, pltpu.roll(lev_pack[1][2:3], last_lev * rows, axis=1), 0.0)
+    ring = ring + jnp.where(at_row == 0, pltpu.roll(lat_pack[0][3:4], cols - last_row, axis=1), 0.0)
+    ring = ring + jnp.where(at_row == last_row, pltpu.roll(lat_pack[1][3:4], last_row, axis=1), 0.0)
+    beside_lon = ends_of(ring * speed_lon)
+
+    below, above = shifted(
+        [lower[k] * field for k in range(3)], [upper[k] * field for k in range(3)],
+        beside_lev, beside_lat, beside_lon,
+    )
+    result = centre * field
+    for k in range(3):
+        result = result + above[k] + below[k]
+    field = result
     adj_v[...] = field
 
     for turn in range(ROUNDS):
         for which in range(6):
             guarded(links[which][2], lambda turn=turn, which=which: message(turn, which).wait_send())
+    for i in range(len(wide_links)):
+        guarded(wide_links[i][1], lambda i=i: wide_message(i).wait_send())
 
 
 def finish(state_v, adj_v, outer, state_hbm, adj_hbm, next_hbm, wide, nxt, out_sem):
@@ -259,7 +409,7 @@
     fine = wide_cols // cols
     lanes = 128
     observed = (obs_column.shape[0] // lanes, lanes)
-    assert 2 * flat_rows <= cols
+    assert 2 * flat_rows == cols and levels > 1 and rows > 1
     f32, bf16 = jnp.float32, jnp.bfloat16
     outer_shape = (levels * outer_rows, wide_cols)
     vmem = pl.BlockSpec(memory_space=pltpu.VMEM)
@@ -285,9 +435,19 @@
             pltpu.VMEM((ROUNDS, 2, rows, cols), f32),
             pltpu.VMEM((ROUNDS, 2, levels, cols), f32),
             pltpu.VMEM((ROUNDS, 2, 1, cols), f32),
+            pltpu.VMEM((2, 2, rows, cols), f32),
+            pltpu.VMEM((2, 2, levels, cols), f32),
+            pltpu.VMEM((4, 2, cols), f32),
+            pltpu.VMEM((4, cols), f32),
+            pltpu.VMEM((2, 2, rows, cols), f32),
+            pltpu.VMEM((2, 2, levels, cols), f32),
+            pltpu.VMEM((4, 2, cols), f32),
+            pltpu.VMEM((10, 4, cols), f32),
             pltpu.SemaphoreType.DMA((5,)),
             pltpu.SemaphoreType.DMA((ROUNDS, 6)),
             pltpu.SemaphoreType.DMA((ROUNDS, 6)),
+            pltpu.SemaphoreType.DMA((18,)),
+            pltpu.SemaphoreType.DMA((18,)),
         ],
         compiler_params=pltpu.CompilerParams(collective_id=0, has_side_effects=True),
     )(

time: 18.6 us -> 17 us (0.914)
  Pallas kernels: 17.8 us -> 16.2 us
    pallas_call x1, Pallas kernels: 16.8 us -> 15.3 us  [shards(): pl.pallas_call(functools.partial(kernel, ends), out_shape=(pltpu.VMEM((le...]
where the time goes in v3:
time: 17 us; the launch traced here: 16.9 us
  Pallas kernels  16.2 us (95%)
  between operations  0.64 us (4%)
    pallas_call x1, Pallas kernels, shards(): pl.pallas_call(functools.partial(kernel, ends), out_shape=(pltpu.VMEM((le...  15.3 us
    pallas_call x1, Pallas kernels, shards(): pl.pallas_call(finish, out_shape=(jax.ShapeDtypeStruct((levels, rows, col...  0.94 us

profile of v3, /device:TPU:0, one launch (start us, length us, event | category | flops | bytes accessed | tf_op | source)
XLA Modules:
  0.0 16.9 jit_solution(9163346197623200990)
XLA Ops:
  0.6 15.3 %shard_map.76 = (f32[4,16,128]{2,1,0:T(8,128)S(1)}, f32[4,16,128]{2,1,0:T(8,128)S(1)}, bf16[256,512]{1,0:T(8,128)(2,1)S(1)}) custom-call(bf16[256,512]{1,0:T(8,128)(2,1)} %bitcast.5, bf16[3,4,16,128]{3,2,1,0:T(8,128)(2,1)} %courant_hbm.1, s32[16,128]{1,0:T(8,128)} %bitcast.6, s32[16,128]{1,0:T(8,128)} %bitcast.7, f32[16,128]{1,0:T(8,128)} %bitcast.8), custom_call_target="tpu_custom_call" | custom-call | tf_op jit(solution)/shard_map/pallas_call | solution.py:417
  15.9 0.9 %shard_map.77 = (f32[4,16,128]{2,1,0:T(8,128)}, f32[4,16,128]{2,1,0:T(8,128)}, bf16[256,512]{1,0:T(8,128)(2,1)}) custom-call(f32[4,16,128]{2,1,0:T(8,128)S(1)} %get-tuple-element.9.state_v, f32[4,16,128]{2,1,0:T(8,128)S(1)} %get-tuple-element.10.adj_v, bf16[256,512]{1,0:T(8,128)(2,1)S(1)} %get-tuple-element.11.outer), custom_call_target="tpu_custom_call" | custom-call | tf_op jit(solution)/shard_map/pallas_call | solution.py:460

commit v4 on v3

--- a/solution.py
+++ b/solution.py
@@ -68,20 +68,20 @@
         wide_links.append((target, exists, joined(*opposite)[1], source, landing))
 
     for s in range(2):
-        add([side_lev[s]], [side_lev[1 - s]], lev2_out.at[s], lev2_in.at[s])
-        add([side_lat[s]], [side_lat[1 - s]], lat2_out.at[s], lat2_in.at[s])
+        add([side_lev[s]], [side_lev[1 - s]], lambda q, s=s: lev2_out.at[q, s], lambda q, s=s: lev2_in.at[q, s])
+        add([side_lat[s]], [side_lat[1 - s]], lambda q, s=s: lat2_out.at[q, s], lambda q, s=s: lat2_in.at[q, s])
     for s in range(2):
         for t in range(2):
             add([side_lev[s], side_lat[t]], [side_lev[1 - s], side_lat[1 - t]],
-                edge_out.at[2 * s + t], edge_in.at[2 * s + t])
+                lambda q, e=2 * s + t: edge_out.at[q, e], lambda q, e=2 * s + t: edge_in.at[q, e])
     faces_end = len(wide_links)
     for u in range(2):
-        add([side_lon[u]], [side_lon[1 - u]], pack_out, pack_in.at[u])
+        add([side_lon[u]], [side_lon[1 - u]], lambda q: pack_out.at[q], lambda q, e=u: pack_in.at[q, e])
     for base, sides in ((2, side_lev), (6, side_lat)):
         for s in range(2):
             for u in range(2):
                 add([sides[s], side_lon[u]], [sides[1 - s], side_lon[1 - u]],
-                    pack_out, pack_in.at[base + 2 * s + u])
+                    lambda q: pack_out.at[q], lambda q, e=base + 2 * s + u: pack_in.at[q, e])
     outs = {"lev": lev_out, "lat": lat_out, "lon": lon_out}
     ins = {"lev": lev_in, "lat": lat_in, "lon": lon_in}
 
@@ -100,19 +100,21 @@
             ),
         )
 
-    def wide_message(i):
+    def wide_message(q, i):
         target, _, _, source, landing = wide_links[i]
         return pltpu.make_async_remote_copy(
-            src_ref=source,
-            dst_ref=landing,
-            send_sem=send2_sem.at[i],
-            recv_sem=recv2_sem.at[i],
+            src_ref=source(q),
+            dst_ref=landing(q),
+            send_sem=send2_sem.at[q, i],
+            recv_sem=recv2_sem.at[q, i],
             device_id=target,
             device_id_type=MESH,
         )
 
     def clear(landing):
-        landing[...] = jnp.zeros(landing.shape, jnp.float32)
+        for q in range(2):
+            ref = landing(q)
+            ref[...] = jnp.zeros(ref.shape, jnp.float32)
 
     for _, _, arrives, _, landing in wide_links:
         if arrives is not None:
@@ -149,13 +151,6 @@
         lax.broadcasted_iota(jnp.int32, (wide_cols, cols), 0) // fine
         == lax.broadcasted_iota(jnp.int32, (wide_cols, cols), 1)
     ).astype(jnp.float32).astype(jnp.bfloat16)
-
-    loads[0].wait()
-    sums[...] = jnp.dot(outer[...], pool, preferred_element_type=jnp.float32)
-    coarse = sums[pl.ds(0, flat_rows, stride=fine), :]
-    for k in range(1, fine):
-        coarse = coarse + sums[pl.ds(k, flat_rows, stride=fine), :]
-    coarse = (coarse * (1.0 / (fine * fine))).reshape(levels, rows, cols)
 
     def pack(first, last):
         first = first.reshape(flat_rows, cols)[:, :1]
@@ -210,15 +205,54 @@
 
     expected = sum(1 if link[1] is None else link[1].astype(jnp.int32) for link in wide_links)
     pl.semaphore_wait(barrier, expected)
-    send(0, [coarse] * 3, [coarse] * 3)
-
     loads[1].wait()
     numbers = courant[...].astype(jnp.float32)
     lower = [jnp.maximum(numbers[k], 0.0) for k in range(3)]
     upper = [jnp.maximum(-numbers[k], 0.0) for k in range(3)]
     centre = 1.0 - jnp.abs(numbers[0]) - jnp.abs(numbers[1]) - jnp.abs(numbers[2])
 
-    send(2, lower, upper)
+    for k in range(3):
+        send(k, [numbers[k]] * 3, [numbers[k]] * 3)
+
+    loads[0].wait()
+    sums[...] = jnp.dot(outer[...], pool, preferred_element_type=jnp.float32)
+    coarse = sums[pl.ds(0, flat_rows, stride=fine), :]
+    for k in range(1, fine):
+        coarse = coarse + sums[pl.ds(k, flat_rows, stride=fine), :]
+    coarse = (coarse * (1.0 / (fine * fine))).reshape(levels, rows, cols)
+
+    lev3 = lax.broadcasted_iota(jnp.int32, (levels, rows, cols), 0)
+    last_lev, last_row = levels - 1, rows - 1
+    lev_edge = (last_lev, 0)
+    row_edge = (last_row, 0)
+    none_lev = jnp.zeros((rows, cols), jnp.float32)
+    none_lat = jnp.zeros((levels, cols), jnp.float32)
+
+    def step(values, lev, lat, lon):
+        below, above = shifted([values] * 3, [values] * 3, lev, lat, lon)
+        result = centre * values
+        for k in range(3):
+            result = result + lower[k] * below[k] + upper[k] * above[k]
+        return result
+
+    partial = step(coarse, [none_lev] * 2, [none_lat] * 2, [0.0, 0.0])
+    for s in range(2):
+        lev2_out[0, s, 0] = partial[lev_edge[s]]
+        lev2_out[0, s, 1] = coarse[lev_edge[s]]
+        lat2_out[0, s, 0] = partial[:, row_edge[s], :]
+        lat2_out[0, s, 1] = coarse[:, row_edge[s], :]
+        for t in range(2):
+            for i in range(2):
+                edge_out[0, 2 * s + t, i : i + 1] = coarse[lev_edge[s], row_edge[t] : row_edge[t] + 1, :]
+    for i in range(faces_end):
+        guarded(wide_links[i][1], lambda i=i: wide_message(0, i).start())
+    own_pack = pack(coarse, coarse)
+    pack_out[0, 0:1] = pack(partial, partial)
+    pack_out[0, 1:2] = own_pack
+    pack_out[0, 2:3] = own_pack
+    pack_out[0, 3:4] = own_pack
+    for i in range(faces_end, len(wide_links)):
+        guarded(wide_links[i][1], lambda i=i: wide_message(0, i).start())
 
     for load in loads[2:]:
         load.wait()
@@ -248,25 +282,77 @@
         + totals[3 * flat_rows :]
     ).reshape(levels, rows, cols)
 
-    def forward(field, turn):
-        lev, lat, lon = receive(turn)
-        below, above = shifted([field] * 3, [field] * 3, lev, lat, ends_of(lon))
-        result = centre * field
-        for k in range(3):
-            result = result + lower[k] * below[k] + upper[k] * above[k]
-        return result
-
-    state = forward(coarse, 0)
-    send(1, [state] * 3, [state] * 3)
-    state = forward(state, 1)
+    plane_row = lax.broadcasted_iota(jnp.int32, (rows, cols), 0)
+    plane_lane = lax.broadcasted_iota(jnp.int32, (rows, cols), 1)
+    line_lev = lax.broadcasted_iota(jnp.int32, (levels, cols), 0)
+    line_lane = lax.broadcasted_iota(jnp.int32, (levels, cols), 1)
+    at_lane = lax.broadcasted_iota(jnp.int32, (1, cols), 1)
+    at = lax.rem(at_lane, flat_rows)
+    at_lev, at_row = lax.div(at, rows), lax.rem(at, rows)
+
+    def packs(q):
+        return (
+            either(pack_in[q, 0], pack_in[q, 1]),
+            [either(pack_in[q, 2 + 2 * s], pack_in[q, 3 + 2 * s]) for s in range(2)],
+            [either(pack_in[q, 6 + 2 * s], pack_in[q, 7 + 2 * s]) for s in range(2)],
+        )
+
+    speeds = [receive(k) for k in range(3)]
+
+    def low(x):
+        return jnp.maximum(x, 0.0)
+
+    def up(x):
+        return jnp.maximum(-x, 0.0)
+
+    for i in range(len(wide_links)):
+        guarded(wide_links[i][2], lambda i=i: wide_message(0, i).wait_recv())
+    side_pack, lev_pack, lat_pack = packs(0)
+    beside_lev, beside_lat = [], []
+    for s in range(2):
+        near, far = (up, low) if s == 0 else (low, up)
+        c = [speeds[k][0][s] for k in range(3)]
+        plane = lev2_in[0, s, 0] + near(c[0]) * coarse[(0, last_lev)[s]]
+        plane = plane + jnp.where(plane_row == 0, low(c[1]) * edge_in[0, 2 * s, 0:1], 0.0)
+        plane = plane + jnp.where(plane_row == last_row, up(c[1]) * edge_in[0, 2 * s + 1, 0:1], 0.0)
+        begin = lev_edge[s] * rows
+        moved = lev_pack[s][1:2]
+        plane = plane + jnp.where(plane_lane == 0, low(c[2]) * column(moved, flat_rows + begin, 1, rows), 0.0)
+        plane = plane + jnp.where(plane_lane == cols - 1, up(c[2]) * column(moved, begin, 1, rows), 0.0)
+        beside_lev.append(plane)
+
+        c = [speeds[k][1][s] for k in range(3)]
+        plane = lat2_in[0, s, 0] + near(c[1]) * coarse[:, (0, last_row)[s], :]
+        plane = plane + jnp.where(line_lev == 0, low(c[0]) * edge_in[0, s, 1:2], 0.0)
+        plane = plane + jnp.where(line_lev == last_lev, up(c[0]) * edge_in[0, 2 + s, 1:2], 0.0)
+        begin = row_edge[s]
+        moved = lat_pack[s][1:2]
+        plane = plane + jnp.where(
+            line_lane == 0, low(c[2]) * column(moved, flat_rows + begin, rows, levels), 0.0
+        )
+        plane = plane + jnp.where(line_lane == cols - 1, up(c[2]) * column(moved, begin, rows, levels), 0.0)
+        beside_lat.append(plane)
+    c = [speeds[k][2] for k in range(3)]
+    ring = side_pack[0:1] + jnp.where(at_lane < flat_rows, low(c[2]), up(c[2])) * pltpu.roll(
+        own_pack, flat_rows, axis=1
+    )
+    turned = [pltpu.roll(lev_pack[0][1:2], cols - last_lev * rows, axis=1), pltpu.roll(lev_pack[1][1:2], last_lev * rows, axis=1)]
+    ring = ring + jnp.where(at_lev == 0, low(c[0]) * turned[0], 0.0)
+    ring = ring + jnp.where(at_lev == last_lev, up(c[0]) * turned[1], 0.0)
+    turned = [pltpu.roll(lat_pack[0][1:2], cols - last_row, axis=1), pltpu.roll(lat_pack[1][1:2], last_row, axis=1)]
+    ring = ring + jnp.where(at_row == 0, low(c[1]) * turned[0], 0.0)
+    ring = ring + jnp.where(at_row == last_row, up(c[1]) * turned[1], 0.0)
+
+    state = step(
+        coarse, [lev2_in[0, s, 1] for s in range(2)], [lat2_in[0, s, 1] for s in range(2)],
+        ends_of(side_pack[1:2]),
+    )
+    state = step(state, beside_lev, beside_lat, ends_of(ring))
     field = count * state - observed
 
     state_v[...] = state
-    lev3 = lax.broadcasted_iota(jnp.int32, (levels, rows, cols), 0)
     to_first = [lower[k] * field for k in range(3)]
     to_last = [upper[k] * field for k in range(3)]
-    none_lev = jnp.zeros((rows, cols), jnp.float32)
-    none_lat = jnp.zeros((levels, cols), jnp.float32)
     below, above = shifted(to_first, to_last, [none_lev] * 2, [none_lat] * 2, [0.0, 0.0])
     partial = centre * field
     for k in range(3):
@@ -277,40 +363,40 @@
     row_edge = (last_row, 0)
     for s in range(2):
         lev_move = (to_last, to_first)[s]
-        lev2_out[s, 0] = partial[lev_edge[s]]
-        lev2_out[s, 1] = lev_move[0][lev_edge[s]]
-        lat2_out[s, 0] = partial[:, row_edge[s], :]
-        lat2_out[s, 1] = lev_move[1][:, row_edge[s], :]
+        lev2_out[1, s, 0] = partial[lev_edge[s]]
+        lev2_out[1, s, 1] = lev_move[0][lev_edge[s]]
+        lat2_out[1, s, 0] = partial[:, row_edge[s], :]
+        lat2_out[1, s, 1] = lev_move[1][:, row_edge[s], :]
         for t in range(2):
             lat_move = (to_last, to_first)[t]
             r = row_edge[t]
-            edge_out[2 * s + t, 0:1] = lat_move[1][lev_edge[s], r : r + 1, :]
-            edge_out[2 * s + t, 1:2] = lev_move[0][lev_edge[s], r : r + 1, :]
+            edge_out[1, 2 * s + t, 0:1] = lat_move[1][lev_edge[s], r : r + 1, :]
+            edge_out[1, 2 * s + t, 1:2] = lev_move[0][lev_edge[s], r : r + 1, :]
     for i in range(faces_end):
-        guarded(wide_links[i][1], lambda i=i: wide_message(i).start())
+        guarded(wide_links[i][1], lambda i=i: wide_message(1, i).start())
     moved_lon = pack(to_first[2], to_last[2])
     at_lev_ends = jnp.where(lev3 == 0, to_first[0], jnp.where(lev3 == last_lev, to_last[0], 0.0))
     at_row_ends = jnp.where(row3 == 0, to_first[1], jnp.where(row3 == last_row, to_last[1], 0.0))
-    pack_out[0:1] = pack(partial, partial)
-    pack_out[1:2] = moved_lon
-    pack_out[2:3] = pack(at_lev_ends, at_lev_ends)
-    pack_out[3:4] = pack(at_row_ends, at_row_ends)
+    pack_out[1, 0:1] = pack(partial, partial)
+    pack_out[1, 1:2] = moved_lon
+    pack_out[1, 2:3] = pack(at_lev_ends, at_lev_ends)
+    pack_out[1, 3:4] = pack(at_row_ends, at_row_ends)
     for i in range(faces_end, len(wide_links)):
-        guarded(wide_links[i][1], lambda i=i: wide_message(i).start())
-
-    speed_lev, speed_lat, speed_lon = receive(2)
+        guarded(wide_links[i][1], lambda i=i: wide_message(1, i).start())
+
+    speed_lev = [up(speeds[0][0][0]), low(speeds[0][0][1])]
+    speed_lat = [up(speeds[1][1][0]), low(speeds[1][1][1])]
+    speed_lon = jnp.where(at_lane < flat_rows, low(speeds[2][2]), up(speeds[2][2]))
     for i in range(len(wide_links)):
-        guarded(wide_links[i][2], lambda i=i: wide_message(i).wait_recv())
-    side_pack = either(pack_in[0], pack_in[1])
-    lev_pack = [either(pack_in[2 + 2 * s], pack_in[3 + 2 * s]) for s in range(2)]
-    lat_pack = [either(pack_in[6 + 2 * s], pack_in[7 + 2 * s]) for s in range(2)]
+        guarded(wide_links[i][2], lambda i=i: wide_message(1, i).wait_recv())
+    side_pack, lev_pack, lat_pack = packs(1)
 
     left, right = ends_of(side_pack[1:2])
     field = partial + jnp.where(lane3 == 0, left, 0.0) + jnp.where(lane3 == cols - 1, right, 0.0)
-    field = field + jnp.where(lev3 == 0, lev2_in[0, 1][None], 0.0)
-    field = field + jnp.where(lev3 == last_lev, lev2_in[1, 1][None], 0.0)
-    field = field + jnp.where(row3 == 0, lat2_in[0, 1][:, None, :], 0.0)
-    field = field + jnp.where(row3 == last_row, lat2_in[1, 1][:, None, :], 0.0)
+    field = field + jnp.where(lev3 == 0, lev2_in[1, 0, 1][None], 0.0)
+    field = field + jnp.where(lev3 == last_lev, lev2_in[1, 1, 1][None], 0.0)
+    field = field + jnp.where(row3 == 0, lat2_in[1, 0, 1][:, None, :], 0.0)
+    field = field + jnp.where(row3 == last_row, lat2_in[1, 1, 1][:, None, :], 0.0)
 
     plane_row = lax.broadcasted_iota(jnp.int32, (rows, cols), 0)
     plane_lane = lax.broadcasted_iota(jnp.int32, (rows, cols), 1)
@@ -319,9 +405,9 @@
     beside_lev, beside_lat = [], []
     for s in range(2):
         own = (to_first[0][0], to_last[0][last_lev])[s]
-        plane = lev2_in[s, 0] + own
-        plane = plane + jnp.where(plane_row == 0, edge_in[2 * s, 0:1], 0.0)
-        plane = plane + jnp.where(plane_row == last_row, edge_in[2 * s + 1, 0:1], 0.0)
+        plane = lev2_in[1, s, 0] + own
+        plane = plane + jnp.where(plane_row == 0, edge_in[1, 2 * s, 0:1], 0.0)
+        plane = plane + jnp.where(plane_row == last_row, edge_in[1, 2 * s + 1, 0:1], 0.0)
         begin = lev_edge[s] * rows
         moved = lev_pack[s][1:2]
         plane = plane + jnp.where(plane_lane == 0, column(moved, flat_rows + begin, 1, rows), 0.0)
@@ -329,9 +415,9 @@
         beside_lev.append(plane * speed_lev[s])
 
         own = (to_first[1][:, 0, :], to_last[1][:, last_row, :])[s]
-        plane = lat2_in[s, 0] + own
-        plane = plane + jnp.where(line_lev == 0, edge_in[s, 1:2], 0.0)
-        plane = plane + jnp.where(line_lev == last_lev, edge_in[2 + s, 1:2], 0.0)
+        plane = lat2_in[1, s, 0] + own
+        plane = plane + jnp.where(line_lev == 0, edge_in[1, s, 1:2], 0.0)
+        plane = plane + jnp.where(line_lev == last_lev, edge_in[1, 2 + s, 1:2], 0.0)
         begin = row_edge[s]
         moved = lat_pack[s][1:2]
         plane = plane + jnp.where(line_lane == 0, column(moved, flat_rows + begin, rows, levels), 0.0)
@@ -359,8 +445,9 @@
     for turn in range(ROUNDS):
         for which in range(6):
             guarded(links[which][2], lambda turn=turn, which=which: message(turn, which).wait_send())
-    for i in range(len(wide_links)):
-        guarded(wide_links[i][1], lambda i=i: wide_message(i).wait_send())
+    for q in range(2):
+        for i in range(len(wide_links)):
+            guarded(wide_links[i][1], lambda q=q, i=i: wide_message(q, i).wait_send())
 
 
 def finish(state_v, adj_v, outer, state_hbm, adj_hbm, next_hbm, wide, nxt, out_sem):
@@ -435,19 +522,19 @@
             pltpu.VMEM((ROUNDS, 2, rows, cols), f32),
             pltpu.VMEM((ROUNDS, 2, levels, cols), f32),
             pltpu.VMEM((ROUNDS, 2, 1, cols), f32),
-            pltpu.VMEM((2, 2, rows, cols), f32),
-            pltpu.VMEM((2, 2, levels, cols), f32),
-            pltpu.VMEM((4, 2, cols), f32),
-            pltpu.VMEM((4, cols), f32),
-            pltpu.VMEM((2, 2, rows, cols), f32),
-            pltpu.VMEM((2, 2, levels, cols), f32),
-            pltpu.VMEM((4, 2, cols), f32),
-            pltpu.VMEM((10, 4, cols), f32),
+            pltpu.VMEM((2, 2, 2, rows, cols), f32),
+            pltpu.VMEM((2, 2, 2, levels, cols), f32),
+            pltpu.VMEM((2, 4, 2, cols), f32),
+            pltpu.VMEM((2, 4, cols), f32),
+            pltpu.VMEM((2, 2, 2, rows, cols), f32),
+            pltpu.VMEM((2, 2, 2, levels, cols), f32),
+            pltpu.VMEM((2, 4, 2, cols), f32),
+            pltpu.VMEM((2, 10, 4, cols), f32),
             pltpu.SemaphoreType.DMA((5,)),
             pltpu.SemaphoreType.DMA((ROUNDS, 6)),
             pltpu.SemaphoreType.DMA((ROUNDS, 6)),
-            pltpu.SemaphoreType.DMA((18,)),
-            pltpu.SemaphoreType.DMA((18,)),
+            pltpu.SemaphoreType.DMA((2, 18)),
+            pltpu.SemaphoreType.DMA((2, 18)),
         ],
         compiler_params=pltpu.CompilerParams(collective_id=0, has_side_effects=True),
     )(

time: 17 us -> 15.5 us (0.912)
  Pallas kernels: 16.2 us -> 14.8 us
    pallas_call x1, Pallas kernels: 15.3 us -> 13.8 us  [shards(): pl.pallas_call(functools.partial(kernel, ends), out_shape=(pltpu.VMEM((le...]
where the time goes in v4:
time: 15.5 us; the launch traced here: 15.4 us
  Pallas kernels  14.8 us (95%)
  between operations  0.64 us (4%)
    pallas_call x1, Pallas kernels, shards(): pl.pallas_call(functools.partial(kernel, ends), out_shape=(pltpu.VMEM((le...  13.8 us
    pallas_call x1, Pallas kernels, shards(): pl.pallas_call(finish, out_shape=(jax.ShapeDtypeStruct((levels, rows, col...  0.94 us

profile of v4, /device:TPU:0, one launch (start us, length us, event | category | flops | bytes accessed | tf_op | source)
XLA Modules:
  0.0 15.4 jit_solution(16938419040865392307)
XLA Ops:
  0.6 13.8 %shard_map.76 = (f32[4,16,128]{2,1,0:T(8,128)S(1)}, f32[4,16,128]{2,1,0:T(8,128)S(1)}, bf16[256,512]{1,0:T(8,128)(2,1)S(1)}) custom-call(bf16[256,512]{1,0:T(8,128)(2,1)} %bitcast.5, bf16[3,4,16,128]{3,2,1,0:T(8,128)(2,1)} %courant_hbm.1, s32[16,128]{1,0:T(8,128)} %bitcast.6, s32[16,128]{1,0:T(8,128)} %bitcast.7, f32[16,128]{1,0:T(8,128)} %bitcast.8), custom_call_target="tpu_custom_call" | custom-call | tf_op jit(solution)/shard_map/pallas_call | solution.py:504
  14.5 0.9 %shard_map.77 = (f32[4,16,128]{2,1,0:T(8,128)}, f32[4,16,128]{2,1,0:T(8,128)}, bf16[256,512]{1,0:T(8,128)(2,1)}) custom-call(f32[4,16,128]{2,1,0:T(8,128)S(1)} %get-tuple-element.9.state_v, f32[4,16,128]{2,1,0:T(8,128)S(1)} %get-tuple-element.10.adj_v, bf16[256,512]{1,0:T(8,128)(2,1)S(1)} %get-tuple-element.11.outer), custom_call_target="tpu_custom_call" | custom-call | tf_op jit(solution)/shard_map/pallas_call | solution.py:547

commit v5 on v4

--- a/solution.py
+++ b/solution.py
@@ -204,15 +204,11 @@
         )
 
     expected = sum(1 if link[1] is None else link[1].astype(jnp.int32) for link in wide_links)
-    pl.semaphore_wait(barrier, expected)
     loads[1].wait()
     numbers = courant[...].astype(jnp.float32)
     lower = [jnp.maximum(numbers[k], 0.0) for k in range(3)]
     upper = [jnp.maximum(-numbers[k], 0.0) for k in range(3)]
     centre = 1.0 - jnp.abs(numbers[0]) - jnp.abs(numbers[1]) - jnp.abs(numbers[2])
-
-    for k in range(3):
-        send(k, [numbers[k]] * 3, [numbers[k]] * 3)
 
     loads[0].wait()
     sums[...] = jnp.dot(outer[...], pool, preferred_element_type=jnp.float32)
@@ -236,6 +232,7 @@
         return result
 
     partial = step(coarse, [none_lev] * 2, [none_lat] * 2, [0.0, 0.0])
+    pl.semaphore_wait(barrier, expected)
     for s in range(2):
         lev2_out[0, s, 0] = partial[lev_edge[s]]
         lev2_out[0, s, 1] = coarse[lev_edge[s]]
@@ -253,6 +250,9 @@
     pack_out[0, 3:4] = own_pack
     for i in range(faces_end, len(wide_links)):
         guarded(wide_links[i][1], lambda i=i: wide_message(0, i).start())
+
+    for k in range(3):
+        send(k, [numbers[k]] * 3, [numbers[k]] * 3)
 
     for load in loads[2:]:
         load.wait()

time: 15.5 us -> 15.1 us (0.974)
  Pallas kernels: 14.8 us -> 14.3 us
    pallas_call x1, Pallas kernels: 13.8 us -> 13.3 us  [shards(): pl.pallas_call(functools.partial(kernel, ends), out_shape=(pltpu.VMEM((le...]
where the time goes in v5:
time: 15.1 us; the launch traced here: 14.9 us
  Pallas kernels  14.3 us (95%)
  between operations  0.64 us (4%)
    pallas_call x1, Pallas kernels, shards(): pl.pallas_call(functools.partial(kernel, ends), out_shape=(pltpu.VMEM((le...  13.3 us
    pallas_call x1, Pallas kernels, shards(): pl.pallas_call(finish, out_shape=(jax.ShapeDtypeStruct((levels, rows, col...  0.94 us

profile of v5, /device:TPU:0, one launch (start us, length us, event | category | flops | bytes accessed | tf_op | source)
XLA Modules:
  0.0 14.9 jit_solution(17077463713012069301)
XLA Ops:
  0.6 13.3 %shard_map.76 = (f32[4,16,128]{2,1,0:T(8,128)S(1)}, f32[4,16,128]{2,1,0:T(8,128)S(1)}, bf16[256,512]{1,0:T(8,128)(2,1)S(1)}) custom-call(bf16[256,512]{1,0:T(8,128)(2,1)} %bitcast.5, bf16[3,4,16,128]{3,2,1,0:T(8,128)(2,1)} %courant_hbm.1, s32[16,128]{1,0:T(8,128)} %bitcast.6, s32[16,128]{1,0:T(8,128)} %bitcast.7, f32[16,128]{1,0:T(8,128)} %bitcast.8), custom_call_target="tpu_custom_call" | custom-call | tf_op jit(solution)/shard_map/pallas_call | solution.py:504
  14.0 0.9 %shard_map.77 = (f32[4,16,128]{2,1,0:T(8,128)}, f32[4,16,128]{2,1,0:T(8,128)}, bf16[256,512]{1,0:T(8,128)(2,1)}) custom-call(f32[4,16,128]{2,1,0:T(8,128)S(1)} %get-tuple-element.9.state_v, f32[4,16,128]{2,1,0:T(8,128)S(1)} %get-tuple-element.10.adj_v, bf16[256,512]{1,0:T(8,128)(2,1)S(1)} %get-tuple-element.11.outer), custom_call_target="tpu_custom_call" | custom-call | tf_op jit(solution)/shard_map/pallas_call | solution.py:547
